TPU v7x, 32 devices: a whole 2x2x4 slice. The times are simulated.
32 devices in a mesh: groups: 1, seq: 32 (over z, y, x, core).
Axes of the slice: x: 2, y: 2, z: 4, core: 2. Of those that a mesh axis runs over, the one named last changes fastest.
Arguments:
- queries: bfloat16 [4096, 4096], P(('groups', 'seq')), may hold values from -100 to 100
- keys_values: bfloat16 [4096, 2, 512], P(('groups', 'seq')), may hold values from -5 to 5
- head_signs: int32 [32, 128], replicated, may hold values from -1 to 1, as said below
- out_codes: int32 [512, 8192], P(None, 'seq'), may hold values from -2147483648 to 2147483647, as said below
- out_scales: bfloat16 [32, 8192], replicated, may hold values from 0.019897461 to 0.19921875
Outputs:
- projected: bfloat16 [4096, 8192], P(('groups', 'seq'))
Inputs may be any that keep to these rules, and one draw needn't show every extreme that they name: `head_signs`: every entry is -1 or 1. `out_codes`: each word holds eight codes of 0 to 15, the code of row 8 i + k in bits 4k to 4k + 3 of word row i, the word read as a signed 32-bit integer.
All inputs are finite; a program needn't handle non-finite values.
Results may differ from a plain program's by a relative error of at most 0.006.
Values may be sent and summed in bfloat16 or wider, within the bound.
A program may use at most 128 MiB of HBM per device.

v0:
```python
import functools
import math

import jax
import jax.numpy as jnp
from jax import lax
from jax.experimental import pallas as pl
from jax.experimental.pallas import tpu as pltpu
from jax.sharding import PartitionSpec as P

HEADS = 32
KV = 4
HD = 128
GROUP = 128
WINDOW = 2048
PLANE = 8
STEPS = 8
PER_STEP = HEADS // STEPS
LOG2E = 1.4426950408889634
MESH = pl.DeviceIdType.MESH
BF16 = jnp.bfloat16
F32 = jnp.float32

TO_COLUMN, TO_X, TO_Y, PASS_Y, PASS_X, TO_CORE = 0, 1, 2, 3, 4, 5
KINDS = 9


def reordered_hadamard():
    column = jnp.arange(HD, dtype=jnp.int32)
    source = (column % 16) * 8 + column // 16
    common = jnp.bitwise_and(jnp.arange(HD, dtype=jnp.int32)[:, None], source[None, :])
    ones = jnp.zeros((HD, HD), jnp.int32)
    for bit in range(HD.bit_length()):
        ones = ones + jnp.bitwise_and(jnp.right_shift(common, bit), 1)
    return jnp.where(ones % 2 == 0, 1.0, -1.0).astype(BF16)


def kernel(
    n, reach,
    q_ref, kv_ref, sign_ref, had_ref, codes_ref, scales_ref, out_ref,
    kvbuf, cbuf, rot, bias, local_sem, kv_send, kv_recv, c_send, c_recv,
):
    rows = q_ref.shape[0]
    cols = codes_ref.shape[1]
    planes = n // PLANE
    back = -(-reach // PLANE)
    me = lax.axis_index("seq")
    z = me // PLANE
    p = me % PLANE
    core, x, y = p % 2, (p // 2) % 2, p // 4
    dx, dy, dc = 2 - 4 * x, 4 - 8 * y, 1 - 2 * core
    px, py, pd = p + dx, p + dy, p + dx + dy

    def column(d):
        return lax.rem(z + d, planes) * PLANE + p

    barrier = pltpu.get_barrier_semaphore()
    peers = [column(d) for d in range(1, planes)] + [me + dx, me + dy, me + dc]
    for peer in peers:
        pl.semaphore_signal(barrier, inc=1, device_id={"seq": peer}, device_id_type=MESH)
    own_kv = pltpu.make_async_copy(kv_ref, kvbuf.at[back * PLANE + p], local_sem.at[0])
    own_codes = pltpu.make_async_copy(codes_ref, cbuf.at[me], local_sem.at[1])
    own_kv.start()
    own_codes.start()

    class Item:
        def __init__(self, buf, base, send, recv):
            self.buf, self.base, self.send, self.recv = buf, base, send, recv
            self.half = buf.shape[1] // 2

        def move(self, kind, d, q, target, part=None, source=None, to=None):
            block = self.buf.at[self.base(d) + q]
            if part is not None:
                block = self.buf.at[self.base(d) + q, pl.ds(part * self.half, self.half)]
            return pltpu.make_async_remote_copy(
                src_ref=block if source is None else source,
                dst_ref=block,
                send_sem=self.send.at[kind, d],
                recv_sem=self.recv.at[kind, d],
                device_id={"seq": target},
                device_id_type=MESH,
            )

        def to_column(self, d, source):
            return self.move(TO_COLUMN, d, p, column(d), source=source)

        def to_x(self, d):
            return self.move(TO_X, d, p, me + dx)

        def to_y(self, d):
            return self.move(TO_Y, d, p, me + dy)

        def pass_y(self, d):
            return self.move(PASS_Y, d, px, me + dy, part=0)

        def pass_x(self, d):
            return self.move(PASS_X, d, py, me + dx, part=1)

        def to_core(self, d, which):
            return self.move(TO_CORE + which, d, (p, px, py, pd)[which], me + dc)

        def stage1(self, d):
            self.to_x(d).start()
            self.to_y(d).start()
            self.to_core(d, 0).start()

        def stage2(self, d):
            self.to_x(d).wait_recv()
            self.pass_y(d).start()
            self.to_core(d, 1).start()
            self.to_y(d).wait_recv()
            self.pass_x(d).start()
            self.to_core(d, 2).start()

        def stage3(self, d):
            self.pass_y(d).wait_recv()
            self.pass_x(d).wait_recv()
            self.to_core(d, 3).start()

        def stage4(self, d):
            for which in range(4):
                self.to_core(d, which).wait_recv()

        def sent(self, d):
            for copy in (self.to_x(d), self.to_y(d), self.pass_y(d), self.pass_x(d)):
                copy.wait_send()
            for which in range(4):
                self.to_core(d, which).wait_send()

    kv = Item(kvbuf, lambda d: (back - d) * PLANE, kv_send, kv_recv)
    codes = Item(cbuf, lambda d: lax.rem(z + planes - d, planes) * PLANE, c_send, c_recv)

    own_kv.wait()
    own_codes.wait()
    pl.semaphore_wait(barrier, len(peers))

    def kv_out(d):
        block = kvbuf.at[back * PLANE + p]
        return pltpu.make_async_remote_copy(
            src_ref=block, dst_ref=kvbuf.at[(back - d) * PLANE + p],
            send_sem=kv_send.at[TO_COLUMN, d], recv_sem=kv_recv.at[TO_COLUMN, d],
            device_id={"seq": column(d)}, device_id_type=MESH,
        )

    def codes_out(d):
        return pltpu.make_async_remote_copy(
            src_ref=cbuf.at[me], dst_ref=cbuf.at[me],
            send_sem=c_send.at[TO_COLUMN, d], recv_sem=c_recv.at[TO_COLUMN, d],
            device_id={"seq": column(d)}, device_id_type=MESH,
        )

    def there(d):
        return z - d >= 0

    near = [d for d in range(1, back + 1) if d < planes]
    for d in near:
        @pl.when(z + d < planes)
        def _():
            kv_out(d).start()
    kv.stage1(0)
    for d in range(1, planes):
        codes_out(d).start()

    for d in range(1, back + 1):
        @pl.when(jnp.logical_not(there(d)))
        def _():
            first = (back - d) * PLANE
            kvbuf[first:first + PLANE] = jnp.zeros((PLANE,) + kvbuf.shape[1:], kvbuf.dtype)

    window_blocks = reach + 1
    first_block = back * PLANE + p - reach
    keys = window_blocks * rows
    query = lax.broadcasted_iota(jnp.int32, (rows, keys), 0)
    key = lax.broadcasted_iota(jnp.int32, (rows, keys), 1) - reach * rows
    gap = query - key
    allowed = (gap >= 0) & (gap < WINDOW) & (key + me * rows >= 0)
    bias[...] = jnp.where(allowed, 0.0, -jnp.inf).astype(F32)

    for d in range(0, back + 1):
        if d in near:
            @pl.when(there(d))
            def _():
                kv_out(d).wait_recv()
                kv.stage1(d)
        if d >= 1 and (d == 1 or d - 1 in near):
            @pl.when(there(d - 1))
            def _():
                kv.stage2(d - 1)
    levels = [0] + near
    @pl.when(there(levels[-1]))
    def _():
        kv.stage2(levels[-1])
    codes.stage1(0)
    for d in levels:
        @pl.when(there(d))
        def _():
            kv.stage3(d)
    for d in levels:
        @pl.when(there(d))
        def _():
            kv.stage4(d)

    def event(j):
        @pl.when(j < planes)
        def _():
            codes_out(j).wait_recv()
            codes.stage1(j)

        @pl.when(j - 1 < planes)
        def _():
            codes.stage2(j - 1)

    def third(d):
        @pl.when(d < planes)
        def _():
            codes.stage3(d)

    def attend(t, carry):
        start = pl.multiple_of(t * (PER_STEP * HD), PER_STEP * HD)
        group = (t * PER_STEP) // (HEADS // KV)
        q = q_ref[:, pl.ds(start, PER_STEP * HD)]
        q = jnp.concatenate([q[:, k * HD:(k + 1) * HD] for k in range(PER_STEP)], axis=0)
        key_lane = pl.multiple_of(group * HD, HD)
        value_lane = pl.multiple_of(group * HD + KV * HD, HD)
        k_rows = kvbuf[pl.ds(first_block, window_blocks), :, pl.ds(key_lane, HD)].reshape(keys, HD)
        v_rows = kvbuf[pl.ds(first_block, window_blocks), :, pl.ds(value_lane, HD)].reshape(keys, HD)
        scores = lax.dot_general(q, k_rows, (((1,), (1,)), ((), ())), preferred_element_type=F32)
        scores = scores.reshape(PER_STEP, rows, keys) * (LOG2E / math.sqrt(HD)) + bias[...][None]
        top = jnp.max(scores, axis=-1, keepdims=True)
        weights = jnp.exp2(scores - top)
        total = jnp.sum(weights, axis=-1, keepdims=True)
        rounded = weights.astype(BF16).reshape(PER_STEP * rows, keys)
        weighted = jnp.dot(rounded, v_rows, preferred_element_type=F32)
        weighted = weighted.reshape(PER_STEP, rows, HD) / total
        signed = weighted * sign_ref[t].astype(F32)[:, None, :]
        signed = signed.reshape(PER_STEP * rows, HD)
        high = signed.astype(BF16)
        low = (signed - high.astype(F32)).astype(BF16)
        mixed = jnp.dot(high, had_ref[...], preferred_element_type=F32)
        mixed = mixed + jnp.dot(low, had_ref[...], preferred_element_type=F32)
        mixed = (mixed * (1.0 / math.sqrt(HD))).astype(BF16)
        for k in range(PER_STEP):
            lanes = pl.ds(pl.multiple_of(start + k * HD, HD), HD)
            rot[:, lanes] = mixed[k * rows:(k + 1) * rows]

        @pl.when(t == 2)
        def _():
            event(1)

        @pl.when(t == 5)
        def _():
            event(2)
            third(0)

        return carry

    lax.fori_loop(0, STEPS, attend, 0)

    chunk_heads = 8
    words = GROUP // 8

    def project(s):
        lanes = pl.ds(pl.multiple_of(s * cols, cols), cols)
        scale = scales_ref[:, lanes]
        acc = jnp.zeros((rows, cols), F32)
        for chunk in range(HEADS // chunk_heads):
            parts = []
            for h in range(chunk * chunk_heads, (chunk + 1) * chunk_heads):
                word = cbuf[s, h * words:(h + 1) * words, :] ^ jnp.int32(-2004318072)
                factor = jnp.broadcast_to(scale[h:h + 1, :], (words, cols))
                for k in range(8):
                    code = jnp.right_shift(jnp.left_shift(word, 28 - 4 * k), 28)
                    parts.append(code.astype(F32).astype(BF16) * factor)
            weight = jnp.concatenate(parts, axis=0)
            piece = rot[:, chunk * chunk_heads * HD:(chunk + 1) * chunk_heads * HD]
            acc = acc + jnp.dot(piece, weight, preferred_element_type=F32)
        out_ref[:, lanes] = acc.astype(BF16)

    def project_some(d, low, high):
        def one(q, c):
            which = q // 2
            project(codes.base(d) + p + (which % 2) * dx + (which // 2) * dy + (q % 2) * dc)
            return c

        lax.fori_loop(low, high, one, 0)

    def finish(j, carry):
        @pl.when(j - 3 < planes)
        def _():
            for which in range(3):
                codes.to_core(j - 3, which).wait_recv()
            project_some(j - 3, 0, 6)

        event(j)

        @pl.when(j >= 4)
        def _():
            third(j - 3)
            codes.to_core(j - 4, 3).wait_recv()
            project_some(j - 4, 6, 8)

        return carry

    lax.fori_loop(3, planes + 4, finish, 0)

    for d in near:
        @pl.when(z + d < planes)
        def _():
            kv_out(d).wait_send()
    for d in levels:
        @pl.when(there(d))
        def _():
            kv.sent(d)
    for d in range(1, planes):
        codes_out(d).wait_send()

    def sent(d, carry):
        codes.sent(d)
        return carry

    lax.fori_loop(0, planes, sent, 0)


def on_device(queries, keys_values, head_signs, out_codes, out_scales):
    n = lax.axis_size("seq")
    rows = queries.shape[0]
    reach = (WINDOW + rows - 2) // rows
    back = -(-reach // PLANE)
    planes = n // PLANE
    word_rows, cols = out_codes.shape
    vmem = pl.BlockSpec(memory_space=pltpu.VMEM)
    dma = pltpu.SemaphoreType.DMA
    return pl.pallas_call(
        functools.partial(kernel, n, reach),
        out_shape=jax.ShapeDtypeStruct((rows, n * cols), BF16),
        in_specs=[vmem] * 6,
        out_specs=vmem,
        scratch_shapes=[
            pltpu.VMEM(((back + 1) * PLANE, rows, 2 * KV * HD), BF16),
            pltpu.VMEM((n, word_rows, cols), jnp.int32),
            pltpu.VMEM((rows, HEADS * HD), BF16),
            pltpu.VMEM((rows, (reach + 1) * rows), F32),
            dma((2,)),
            dma((KINDS, back + 1)),
            dma((KINDS, back + 1)),
            dma((KINDS, planes)),
            dma((KINDS, planes)),
        ],
        compiler_params=pltpu.CompilerParams(
            collective_id=0, has_side_effects=True, vmem_limit_bytes=64 * 1000 * 1000
        ),
    )(
        queries,
        keys_values.reshape(rows, 2 * KV * HD),
        head_signs.reshape(STEPS, PER_STEP, HD),
        reordered_hadamard(),
        out_codes,
        out_scales,
    )


def solution(mesh):
    return jax.shard_map(
        on_device,
        mesh=mesh,
        in_specs=(
            P(("groups", "seq"), None),
            P(("groups", "seq"), None, None),
            P(),
            P(None, "seq"),
            P(),
        ),
        out_specs=P(("groups", "seq"), None),
        check_vma=False,
    )
```

profile of v0, /device:TPU:17, one launch (start us, length us, event | category | flops | bytes accessed | tf_op | source)
XLA Modules:
  0.0 128.7 jit_solution(2958016778470971778)
XLA Ops:
  0.0 0.7 select_convert_fusion.had_ref
  0.7 1.7 %copy.6 = bf16[16,8,2,512]{3,1,2,0:T(8,128)(2,1)} copy(bf16[16,8,2,512]{3,2,1,0:T(2,128)(2,1)} %bitcast.4) | data formatting | bytes 524288
  2.4 123.2 %shard_map.55 = bf16[128,8192]{1,0:T(8,128)(2,1)} custom-call(bf16[128,4096]{1,0:T(8,128)(2,1)} %q_ref.1, bf16[128,1024]{1,0:T(8,128)(2,1)} %bitcast.3, s32[8,4,128]{2,1,0:T(4,128)} %bitcast.5, bf16[128,128]{1,0:T(8,128)(2,1)} %select_convert_fusion.had_ref, s32[512,256]{1,0:T(8,128)} %codes_ref.1, bf16[32,8192]{1,0:T(8,128)(2,1)} %scales_ref.1), custom_call_target="tpu_custom_call" | custom-call | tf_op jit(solution)/shard_map/pallas_call | solution.py:333
  125.6 3.1 %copy.8 = bf16[128,8192]{1,0:T(8,128)(2,1)} copy(bf16[128,8192]{1,0:T(8,128)(2,1)} %shard_map.55) | data formatting | bytes 4194304
  (1 shorter events, 0.0 us)
where the time goes:
time: 129 us
  Pallas kernels  123 us (95%)
  local copies, waits for them, and re-layouts  4.78 us (4%)
    pallas_call x1, Pallas kernels, on_device(): pl.pallas_call(functools.partial(kernel, n, reach), out_shape=jax.ShapeDt...  123 us
    unnamed x2, local copies, waits for them, and re-layouts  4.78 us

commit v1 on v0

v1 whole, which is shorter than its diff:
```python
import functools
import math

import jax
import jax.numpy as jnp
from jax import lax
from jax.experimental import pallas as pl
from jax.experimental.pallas import tpu as pltpu
from jax.sharding import PartitionSpec as P

HEADS = 32
KV = 4
HD = 128
GROUP = 128
WINDOW = 2048
QUAD = 4
LANE_HEADS = HEADS // QUAD
HALVES = 2
PER_STEP = LANE_HEADS // HALVES
STEPS = QUAD * HALVES
LOG2E = 1.4426950408889634
MESH = pl.DeviceIdType.MESH
BF16 = jnp.bfloat16
F32 = jnp.float32


def reordered_hadamard():
    column = jnp.arange(HD, dtype=jnp.int32)
    source = (column % 16) * 8 + column // 16
    common = jnp.bitwise_and(jnp.arange(HD, dtype=jnp.int32)[:, None], source[None, :])
    ones = jnp.zeros((HD, HD), jnp.int32)
    for bit in range(HD.bit_length()):
        ones = ones + jnp.bitwise_and(jnp.right_shift(common, bit), 1)
    return jnp.where(ones % 2 == 0, 1.0, -1.0).astype(BF16)


def kernel(
    n, reach, slots,
    q_ref, kv_ref, sign_ref, had_ref, codes_ref, scales_ref, out_ref,
    win, ones, qbuf, cbuf, rot, bias, stage, local_sem,
    kq_s, kq_r, qs, qr, zs, zr, ys, yr, up_s, up_r, dn_s, dn_r, cy_s, cy_r,
    rx_s, rx_r, rc_s, rc_r, rf_s, rf_r, os, orr, ol,
):
    rows = q_ref.shape[0]
    cols = codes_ref.shape[1]
    planes = n // (2 * QUAD)
    width = LANE_HEADS * HD
    half_width = PER_STEP * HD
    top_slot = slots - 1
    me = lax.axis_index("seq")
    z = me // (2 * QUAD)
    y = (me // QUAD) % 2
    lane = me % QUAD
    quad = me // QUAD
    core, x = lane % 2, lane // 2
    dc, dx, dy = 1 - 2 * core, 2 - 4 * x, QUAD - 2 * QUAD * y
    up, down = me + 2 * QUAD, me - 2 * QUAD
    has_up, has_down = z + 1 < planes, z >= 1

    def off(k):
        return (k % 2) * dc + (k // 2) * dx

    def remote(src, dst, send, recv, target):
        return pltpu.make_async_remote_copy(
            src_ref=src, dst_ref=dst, send_sem=send, recv_sem=recv,
            device_id={"seq": target}, device_id_type=MESH,
        )

    barrier = pltpu.get_barrier_semaphore()

    def greet(target):
        pl.semaphore_signal(barrier, inc=1, device_id={"seq": target}, device_id_type=MESH)

    for k in (2, 3, 1):
        greet(me + off(k))
    greet(me + dy)

    @pl.when(has_up)
    def _():
        greet(up)

    @pl.when(has_down)
    def _():
        greet(down)

    own_kv = pltpu.make_async_copy(
        kv_ref.at[lane], win.at[top_slot * QUAD + lane, :, pl.ds(0, 2 * HD)], local_sem.at[0])
    own_lanes = pl.ds(pl.multiple_of(lane * width, width), width)
    own_q = pltpu.make_async_copy(q_ref.at[:, own_lanes], qbuf.at[0], local_sem.at[1])
    own_codes = pltpu.make_async_copy(codes_ref, cbuf.at[quad], local_sem.at[2])
    own_kv.start()
    own_q.start()
    own_codes.start()

    pl.semaphore_wait(barrier, QUAD + has_up.astype(jnp.int32) + has_down.astype(jnp.int32))

    def block(slot, k):
        return win.at[slot * QUAD + lane + off(k), :, pl.ds(0, 2 * HD)]

    def kv_quad(k):
        return remote(kv_ref.at[lane + off(k)], win.at[top_slot * QUAD + lane, :, pl.ds(0, 2 * HD)],
                      kq_s.at[k], kq_r.at[k], me + off(k))

    def kv_quad_in(k):
        return remote(block(top_slot, k), block(top_slot, k), kq_s.at[k], kq_r.at[k], me + off(k))

    def source(slot, k):
        return kv_ref.at[lane] if slot == top_slot and k == 0 else block(slot, k)

    def z_kv(slot, k):
        return remote(source(slot, k), block(slot - 2, k),
                      zs.at[(top_slot - slot) // 2, k], zr.at[(top_slot - slot) // 2, k], up)

    def y_kv(slot, target, k):
        level = (top_slot - 1 - target) // 2
        return remote(source(slot, k), block(target, k), ys.at[level, k], yr.at[level, k], me + dy)

    def there(slot):
        return quad - top_slot + slot >= 0

    def forward_kv(slot, k, act):
        if slot >= 2:
            @pl.when(there(slot) & has_up)
            def _():
                act(z_kv(slot, k))
        if slot >= 1:
            @pl.when(there(slot) & (y == 0))
            def _():
                act(y_kv(slot, slot - 1, k))
        if slot + 1 < top_slot:
            @pl.when(there(slot) & (y == 1))
            def _():
                act(y_kv(slot, slot + 1, k))

    def q_quad(k):
        lanes = pl.ds(pl.multiple_of((lane + off(k)) * width, width), width)
        return remote(q_ref.at[:, lanes], qbuf.at[k], qs.at[k], qr.at[k], me + off(k))

    def code_up(k):
        unit = cbuf.at[quad - 2 * k] if not isinstance(k, int) or k > 0 else codes_ref
        return remote(unit, cbuf.at[quad - 2 * k], up_s.at[k + 1], up_r.at[k + 1], up)

    def code_up_in(k):
        unit = cbuf.at[quad - 2 * k]
        return remote(unit, unit, up_s.at[k], up_r.at[k], up)

    def code_down(k):
        unit = cbuf.at[quad + 2 * k] if not isinstance(k, int) or k > 0 else codes_ref
        return remote(unit, cbuf.at[quad + 2 * k], dn_s.at[k + 1], dn_r.at[k + 1], down)

    def code_down_in(k):
        unit = cbuf.at[quad + 2 * k]
        return remote(unit, unit, dn_s.at[k], dn_r.at[k], down)

    def code_y(plane):
        unit = cbuf.at[plane * 2 + y]
        return remote(unit, unit, cy_s.at[plane], cy_r.at[plane], me + dy)

    def code_y_in(plane):
        unit = cbuf.at[plane * 2 + 1 - y]
        return remote(unit, unit, cy_s.at[plane], cy_r.at[plane], me + dy)

    for k in (2, 3, 1):
        kv_quad(k).start()
    forward_kv(top_slot, 0, lambda copy: copy.start())

    @pl.when(has_down)
    def _():
        code_down(0).start()
    for k in (1, 2, 3):
        q_quad(k).start()

    window_blocks = reach + 1
    keys = window_blocks * rows
    query = lax.broadcasted_iota(jnp.int32, (rows, keys), 0)
    key = lax.broadcasted_iota(jnp.int32, (rows, keys), 1) - reach * rows
    gap = query - key
    bias[...] = jnp.where((gap >= 0) & (gap < WINDOW), 0.0, -jnp.inf).astype(F32)
    for slot in range(slots):
        value = jnp.where(there(slot), 1.0, 0.0).astype(F32)
        ones[slot * QUAD:(slot + 1) * QUAD] = jnp.full((QUAD, rows, HD), value, F32).astype(BF16)

    for k in (1, 2, 3):
        kv_quad_in(k).wait_recv()
        forward_kv(top_slot, k, lambda copy: copy.start())
    own_kv.wait()
    for slot in range(top_slot - 2, -1, -2):
        for k in range(QUAD):
            @pl.when(there(slot))
            def _():
                z_kv(slot + 2, k).wait_recv()
            forward_kv(slot, k, lambda copy: copy.start())

    own_codes.wait()

    @pl.when(has_up)
    def _():
        code_up(0).start()
    code_y(z).start()

    for slot in range(top_slot):
        @pl.when(jnp.logical_not(there(slot)))
        def _():
            first = win[top_slot * QUAD, 0:1, 0:HD].astype(F32)
            fill = jnp.concatenate([jnp.broadcast_to(first, (rows, HD)), jnp.zeros((rows, HD), F32)], axis=1)
            fill = fill.astype(BF16)
            for i in range(QUAD):
                win[slot * QUAD + i] = fill

    for slot in range(top_slot - 1, -1, -2):
        for k in range(QUAD):
            @pl.when(there(slot))
            def _():
                level = (top_slot - 1 - slot) // 2
                remote(block(slot, k), block(slot, k), ys.at[level, k], yr.at[level, k], me + dy).wait_recv()
    own_q.wait()

    def relay(k):
        @pl.when(z - k >= 0)
        def _():
            code_up_in(k).wait_recv()

            @pl.when(has_up)
            def _():
                code_up(k).start()
            code_y(z - k).start()

        @pl.when(z + k < planes)
        def _():
            code_down_in(k).wait_recv()

            @pl.when(has_down)
            def _():
                code_down(k).start()
            code_y(z + k).start()

    def piece(r, source_lane, half):
        start = source_lane * width + half * half_width
        return rot.at[r, :, pl.ds(pl.multiple_of(start, half_width), half_width)]

    def rot_x(t):
        ref = piece(lane + off(t // 2), lane, t % 2)
        return remote(ref, ref, rx_s.at[t], rx_r.at[t], me + dx)

    def rot_c(t):
        ref = piece(lane + off(t // 2), lane, t % 2)
        return remote(ref, ref, rc_s.at[t], rc_r.at[t], me + dc)

    def rot_x_in(t):
        k = t // 2
        ref = piece(lane + dx + (k % 2) * dc - (k // 2) * dx, lane + dx, t % 2)
        return remote(ref, ref, rx_s.at[t], rx_r.at[t], me + dx)

    def rot_f(t):
        k = t // 2
        ref = piece(lane + dx + (k % 2) * dc - (k // 2) * dx, lane + dx, t % 2)
        return remote(ref, ref, rf_s.at[t], rf_r.at[t], me + dc)

    def rot_c_in(t):
        k = t // 2
        ref = piece(lane + dc - (k % 2) * dc + (k // 2) * dx, lane + dc, t % 2)
        return remote(ref, ref, rc_s.at[t], rc_r.at[t], me + dc)

    def rot_f_in(t):
        k = t // 2
        ref = piece(lane + dc + dx - (k % 2) * dc - (k // 2) * dx, lane + dc + dx, t % 2)
        return remote(ref, ref, rf_s.at[t], rf_r.at[t], me + dc)

    def attend(t, carry):
        k = t // HALVES
        half = t % HALVES
        r = lane + off(k)

        @pl.when((half == 0) & (k > 0))
        def _():
            remote(qbuf.at[k], qbuf.at[k], qs.at[k], qr.at[k], me + off(k)).wait_recv()

        lanes = pl.ds(pl.multiple_of(half * half_width, half_width), half_width)
        q = qbuf[k, :, lanes]
        q = jnp.concatenate([q[:, h * HD:(h + 1) * HD] for h in range(PER_STEP)], axis=0)
        k_rows = win[pl.ds(r, window_blocks), :, 0:HD].reshape(keys, HD)
        v_rows = win[pl.ds(r, window_blocks), :, HD:2 * HD].reshape(keys, HD)
        v_rows = jnp.concatenate([v_rows, ones[pl.ds(r, window_blocks)].reshape(keys, HD)], axis=1)
        scores = lax.dot_general(q, k_rows, (((1,), (1,)), ((), ())), preferred_element_type=F32)
        scores = scores.reshape(PER_STEP, rows, keys) * (LOG2E / math.sqrt(HD)) + bias[...][None]
        top = jnp.max(scores, axis=-1, keepdims=True)
        weights = jnp.exp2(scores - top).astype(BF16)
        weighted = jnp.dot(weights.reshape(PER_STEP * rows, keys), v_rows, preferred_element_type=F32)
        weighted = weighted[:, :HD] / weighted[:, HD:]
        signs = sign_ref[lane * HALVES + half].astype(F32)
        signed = weighted.reshape(PER_STEP, rows, HD) * signs[:, None, :]
        signed = signed.reshape(PER_STEP * rows, HD)
        high = signed.astype(BF16)
        low = (signed - high.astype(F32)).astype(BF16)
        mixed = jnp.dot(high, had_ref[...], preferred_element_type=F32)
        mixed = mixed + jnp.dot(low, had_ref[...], preferred_element_type=F32)
        mixed = (mixed * (1.0 / math.sqrt(HD))).astype(BF16)
        start = lane * width + half * half_width
        for h in range(PER_STEP):
            rot[r, :, pl.ds(pl.multiple_of(start + h * HD, HD), HD)] = mixed[h * rows:(h + 1) * rows]

        @pl.when(t >= 1)
        def _():
            rot_x_in(t - 1).wait_recv()
            rot_f(t - 1).start()

        @pl.when(t == 3)
        def _():
            relay(1)

        @pl.when(t == 6)
        def _():
            relay(2)

        rot_x(t).start()
        rot_c(t).start()
        return carry

    lax.fori_loop(0, STEPS, attend, 0)
    rot_x_in(STEPS - 1).wait_recv()
    rot_f(STEPS - 1).start()

    def gathered(t, carry):
        rot_c_in(t).wait_recv()
        rot_f_in(t).wait_recv()
        return carry

    lax.fori_loop(0, STEPS, gathered, 0)

    chunk_heads = 8
    words = GROUP // 8

    def lanes_of(unit, source_lane):
        s = unit * QUAD + source_lane
        return pl.ds(pl.multiple_of(s * cols, cols), cols)

    def out_send(unit, k):
        target = out_ref.at[:, lanes_of(unit, lane)]
        return remote(stage.at[unit, lane + off(k)], target, os.at[unit, k], orr.at[unit, k], me + off(k))

    def out_recv(unit, k):
        target = out_ref.at[:, lanes_of(unit, lane + off(k))]
        return remote(target, target, os.at[unit, k], orr.at[unit, k], me + off(k))

    def out_own(unit):
        return pltpu.make_async_copy(stage.at[unit, lane], out_ref.at[:, lanes_of(unit, lane)], ol.at[unit])

    def project(unit):
        scale = scales_ref[:, lanes_of(unit, lane)]
        acc = jnp.zeros((QUAD * rows, cols), F32)
        for chunk in range(HEADS // chunk_heads):
            parts = []
            for h in range(chunk * chunk_heads, (chunk + 1) * chunk_heads):
                word = cbuf[unit, h * words:(h + 1) * words, :] ^ jnp.int32(-2004318072)
                factor = jnp.broadcast_to(scale[h:h + 1, :], (words, cols))
                for k in range(8):
                    code = jnp.right_shift(jnp.left_shift(word, 28 - 4 * k), 28)
                    parts.append(code.astype(F32).astype(BF16) * factor)
            weight = jnp.concatenate(parts, axis=0)
            span = chunk_heads * HD
            lhs = rot[:, :, chunk * span:(chunk + 1) * span].reshape(QUAD * rows, span)
            acc = acc + jnp.dot(lhs, weight, preferred_element_type=F32)
        acc = acc.astype(BF16).reshape(QUAD, rows, cols)
        stage[unit] = acc
        for k in (2, 3, 1):
            out_send(unit, k).start()
        out_own(unit).start()

    def sweep(k, carry):
        @pl.when(k >= 3)
        def _():
            relay(k)

        def one(j, inner):
            side, other = j // 2, j % 2
            plane = z + k * (2 * side - 1)

            @pl.when((plane >= 0) & (plane < planes) & ((k > 0) | (side == 0)))
            def _():
                @pl.when(other == 1)
                def _():
                    code_y_in(plane).wait_recv()
                project(plane * 2 + y + other * (1 - 2 * y))

            return inner

        lax.fori_loop(0, 4, one, 0)
        return carry

    lax.fori_loop(0, planes, sweep, 0)

    for k in (1, 2, 3):
        kv_quad(k).wait_send()
        q_quad(k).wait_send()
    for slot in range(top_slot, -1, -2):
        for k in range(QUAD):
            forward_kv(slot, k, lambda copy: copy.wait_send())

    def drain_codes(k, carry):
        @pl.when((z - k >= 0) & has_up)
        def _():
            code_up(k).wait_send()

        @pl.when((z + k < planes) & has_down)
        def _():
            code_down(k).wait_send()
        code_y(k).wait_send()
        return carry

    lax.fori_loop(0, planes, drain_codes, 0)

    def drain_rot(t, carry):
        rot_x(t).wait_send()
        rot_c(t).wait_send()
        rot_f(t).wait_send()
        return carry

    lax.fori_loop(0, STEPS, drain_rot, 0)

    def drain_out(unit, carry):
        out_own(unit).wait()
        for k in (1, 2, 3):
            out_send(unit, k).wait_send()
            out_recv(unit, k).wait_recv()
        return carry

    lax.fori_loop(0, 2 * planes, drain_out, 0)


def on_device(queries, keys_values, head_signs, out_codes, out_scales):
    n = lax.axis_size("seq")
    rows = queries.shape[0]
    reach = (WINDOW + rows - 2) // rows
    span = -(-reach // QUAD)
    slots = span + 1
    assert slots % 2 == 1
    planes = n // (2 * QUAD)
    word_rows, cols = out_codes.shape
    vmem = pl.BlockSpec(memory_space=pltpu.VMEM)
    dma = pltpu.SemaphoreType.DMA
    per_head = keys_values.reshape(rows, 2, KV, HD).transpose(2, 0, 1, 3).reshape(KV, rows, 2 * HD)
    return pl.pallas_call(
        functools.partial(kernel, n, reach, slots),
        out_shape=jax.ShapeDtypeStruct((rows, n * cols), BF16),
        in_specs=[vmem] * 6,
        out_specs=pl.BlockSpec(memory_space=pl.ANY),
        scratch_shapes=[
            pltpu.VMEM((slots * QUAD, rows, 2 * HD), BF16),
            pltpu.VMEM((slots * QUAD, rows, HD), BF16),
            pltpu.VMEM((QUAD, rows, LANE_HEADS * HD), BF16),
            pltpu.VMEM((2 * planes, word_rows, cols), jnp.int32),
            pltpu.VMEM((QUAD, rows, HEADS * HD), BF16),
            pltpu.VMEM((rows, (reach + 1) * rows), F32),
            pltpu.VMEM((2 * planes, QUAD, rows, cols), BF16),
            dma((3,)),
            dma((QUAD,)), dma((QUAD,)),
            dma((QUAD,)), dma((QUAD,)),
            dma((slots // 2, QUAD)), dma((slots // 2, QUAD)),
            dma((slots // 2, QUAD)), dma((slots // 2, QUAD)),
            dma((planes + 1,)), dma((planes + 1,)),
            dma((planes + 1,)), dma((planes + 1,)),
            dma((planes,)), dma((planes,)),
            dma((STEPS,)), dma((STEPS,)),
            dma((STEPS,)), dma((STEPS,)),
            dma((STEPS,)), dma((STEPS,)),
            dma((2 * planes, QUAD)), dma((2 * planes, QUAD)),
            dma((2 * planes,)),
        ],
        compiler_params=pltpu.CompilerParams(
            collective_id=0, has_side_effects=True, vmem_limit_bytes=64 * 1000 * 1000
        ),
    )(
        queries,
        per_head,
        head_signs.reshape(STEPS, PER_STEP, HD),
        reordered_hadamard(),
        out_codes,
        out_scales,
    )


def solution(mesh):
    return jax.shard_map(
        on_device,
        mesh=mesh,
        in_specs=(
            P(("groups", "seq"), None),
            P(("groups", "seq"), None, None),
            P(),
            P(None, "seq"),
            P(),
        ),
        out_specs=P(("groups", "seq"), None),
        check_vma=False,
    )
```

time: 129 us -> 95.9 us (0.74); the launches traced: 129 us -> 94.1 us
  Pallas kernels: 123 us -> 89 us
    pallas_call x1, Pallas kernels: 123 us -> 89 us  [on_device(): pl.pallas_call(functools.partial(kernel, n, reach, slots), out_shape=jax....]
    unnamed x2 -> x3, local copies, waits for them, and re-layouts: 4.78 us -> 3.33 us
where the time goes in v1:
time: 95.9 us; the launch traced here: 94.1 us
  Pallas kernels  89 us (93%)
  local copies, waits for them, and re-layouts  4.38 us (5%)
    pallas_call x1, Pallas kernels, on_device(): pl.pallas_call(functools.partial(kernel, n, reach, slots), out_shape=jax....  89 us
    unnamed x3, local copies, waits for them, and re-layouts  3.33 us

profile of v1, /device:TPU:17, one launch (start us, length us, event | category | flops | bytes accessed | tf_op | source)
XLA Modules:
  0.0 94.1 jit_solution(8384253022745408161)
XLA Ops:
  0.0 0.0 copy-start
  0.0 0.7 select_convert_fusion.had_ref
  0.7 0.2 copy-done
  1.0 0.2 bitcast_bitcast_fusion
  1.1 0.9 reshape.32.kv_ref
  2.0 89.0 %shard_map.55 = bf16[128,8192]{1,0:T(8,128)(2,1)} custom-call(bf16[128,4096]{1,0:T(8,128)(2,1)} %q_ref.1, bf16[4,128,256]{2,1,0:T(8,128)(2,1)} %reshape.32.kv_ref, s32[8,4,128]{2,1,0:T(4,128)} %bitcast.8, bf16[128,128]{1,0:T(8,128)(2,1)} %select_convert_fusion.had_ref, s32[512,256]{1,0:T(8,128)} %codes_ref.1, bf16[32,8192]{1,0:T(8,128)(2,1)} %scales_ref.1), custom_call_target="tpu_custom_call" | custom-call | tf_op jit(solution)/shard_map/pallas_call | solution.py:442
  91.0 3.1 %copy.10 = bf16[128,8192]{1,0:T(8,128)(2,1)} copy(bf16[128,8192]{1,0:T(8,128)(2,1)} %shard_map.55) | data formatting | bytes 4194304
  (1 shorter events, 0.0 us)
Async XLA Ops:
  0.0 1.0 %copy-start = (bf16[128,2,512]{2,1,0:T(2,128)(2,1)S(1)}, bf16[128,2,512]{2,1,0:T(2,128)(2,1)}, u32[]{:S(2)}) copy-start(bf16[128,2,512]{2,1,0:T(2,128)(2,1)} %param.6) | copy-start | bytes 786436

commit v2 on v1

--- a/solution.py
+++ b/solution.py
@@ -18,6 +18,7 @@
 HALVES = 2
 PER_STEP = LANE_HEADS // HALVES
 STEPS = QUAD * HALVES
+LAG = 3
 LOG2E = 1.4426950408889634
 MESH = pl.DeviceIdType.MESH
 BF16 = jnp.bfloat16
@@ -160,6 +161,43 @@
         unit = cbuf.at[plane * 2 + 1 - y]
         return remote(unit, unit, cy_s.at[plane], cy_r.at[plane], me + dy)
 
+    near = jnp.minimum(z, planes - 1 - z)
+    toward = jnp.where(z <= planes - 1 - z, 1, -1)
+
+    def plane_at(p):
+        both = z + ((p + 1) // 2) * (2 * (p % 2) - 1)
+        return jnp.where(p <= 2 * near, both, z + toward * (p - near))
+
+    begin = jnp.where(z == 0, 125, jnp.where(z == 1, 186, jnp.where(z == 2, 220, 200)))
+    due = [None]
+    for p in range(1, planes):
+        d = plane_at(p) - z
+        arrival = jnp.where(d > 0, 53 + 130 * d, jnp.where(z == 1, 123, 183) - 117 * d)
+        step = jnp.maximum((arrival - begin - 17) // 33, 0)
+        step = jnp.where((d == 1) & has_down, -1, step)
+        due.append(step if p == 1 else jnp.maximum(due[-1], step))
+
+    def relay(p):
+        plane = plane_at(p)
+
+        @pl.when(plane < z)
+        def _():
+            code_up_in(z - plane).wait_recv()
+
+            @pl.when(has_up)
+            def _():
+                code_up(z - plane).start()
+            code_y(plane).start()
+
+        @pl.when(plane > z)
+        def _():
+            code_down_in(plane - z).wait_recv()
+
+            @pl.when(has_down)
+            def _():
+                code_down(plane - z).start()
+            code_y(plane).start()
+
     for k in (2, 3, 1):
         kv_quad(k).start()
     forward_kv(top_slot, 0, lambda copy: copy.start())
@@ -190,13 +228,22 @@
             def _():
                 z_kv(slot + 2, k).wait_recv()
             forward_kv(slot, k, lambda copy: copy.start())
-
-    own_codes.wait()
-
-    @pl.when(has_up)
-    def _():
-        code_up(0).start()
-    code_y(z).start()
+        if slot in (top_slot - 2, 0):
+            if slot == top_slot - 2:
+                own_codes.wait()
+
+                @pl.when(has_up)
+                def _():
+                    code_up(0).start()
+
+            @pl.when(y == (0 if slot == top_slot - 2 else 1))
+            def _():
+                code_y(z).start()
+
+    for p in range(1, planes):
+        @pl.when(due[p] < 0)
+        def _():
+            relay(p)
 
     for slot in range(top_slot):
         @pl.when(jnp.logical_not(there(slot)))
@@ -214,25 +261,6 @@
                 level = (top_slot - 1 - slot) // 2
                 remote(block(slot, k), block(slot, k), ys.at[level, k], yr.at[level, k], me + dy).wait_recv()
     own_q.wait()
-
-    def relay(k):
-        @pl.when(z - k >= 0)
-        def _():
-            code_up_in(k).wait_recv()
-
-            @pl.when(has_up)
-            def _():
-                code_up(k).start()
-            code_y(z - k).start()
-
-        @pl.when(z + k < planes)
-        def _():
-            code_down_in(k).wait_recv()
-
-            @pl.when(has_down)
-            def _():
-                code_down(k).start()
-            code_y(z + k).start()
 
     def piece(r, source_lane, half):
         start = source_lane * width + half * half_width
@@ -299,34 +327,31 @@
         for h in range(PER_STEP):
             rot[r, :, pl.ds(pl.multiple_of(start + h * HD, HD), HD)] = mixed[h * rows:(h + 1) * rows]
 
-        @pl.when(t >= 1)
-        def _():
-            rot_x_in(t - 1).wait_recv()
-            rot_f(t - 1).start()
-
-        @pl.when(t == 3)
-        def _():
-            relay(1)
-
-        @pl.when(t == 6)
-        def _():
-            relay(2)
+        @pl.when(t >= LAG)
+        def _():
+            rot_x_in(t - LAG).wait_recv()
+            rot_f(t - LAG).start()
+
+        for p in range(1, planes):
+            @pl.when(t == due[p])
+            def _():
+                relay(p)
 
         rot_x(t).start()
         rot_c(t).start()
         return carry
 
     lax.fori_loop(0, STEPS, attend, 0)
-    rot_x_in(STEPS - 1).wait_recv()
-    rot_f(STEPS - 1).start()
-
     def gathered(t, carry):
         rot_c_in(t).wait_recv()
+        return carry
+
+    def gathered_far(t, carry):
         rot_f_in(t).wait_recv()
         return carry
 
     lax.fori_loop(0, STEPS, gathered, 0)
-
+    lax.fori_loop(0, STEPS // 2, gathered_far, 0)
     chunk_heads = 8
     words = GROUP // 8
 
@@ -345,9 +370,9 @@
     def out_own(unit):
         return pltpu.make_async_copy(stage.at[unit, lane], out_ref.at[:, lanes_of(unit, lane)], ol.at[unit])
 
-    def project(unit):
+    def project(unit, side):
         scale = scales_ref[:, lanes_of(unit, lane)]
-        acc = jnp.zeros((QUAD * rows, cols), F32)
+        acc = jnp.zeros((2 * rows, cols), F32)
         for chunk in range(HEADS // chunk_heads):
             parts = []
             for h in range(chunk * chunk_heads, (chunk + 1) * chunk_heads):
@@ -358,36 +383,49 @@
                     parts.append(code.astype(F32).astype(BF16) * factor)
             weight = jnp.concatenate(parts, axis=0)
             span = chunk_heads * HD
-            lhs = rot[:, :, chunk * span:(chunk + 1) * span].reshape(QUAD * rows, span)
+            lhs = rot[pl.ds(2 * side, 2), :, chunk * span:(chunk + 1) * span].reshape(2 * rows, span)
             acc = acc + jnp.dot(lhs, weight, preferred_element_type=F32)
-        acc = acc.astype(BF16).reshape(QUAD, rows, cols)
-        stage[unit] = acc
-        for k in (2, 3, 1):
-            out_send(unit, k).start()
-        out_own(unit).start()
-
-    def sweep(k, carry):
-        @pl.when(k >= 3)
-        def _():
-            relay(k)
-
-        def one(j, inner):
-            side, other = j // 2, j % 2
-            plane = z + k * (2 * side - 1)
-
-            @pl.when((plane >= 0) & (plane < planes) & ((k > 0) | (side == 0)))
-            def _():
-                @pl.when(other == 1)
+        stage[unit, pl.ds(2 * side, 2)] = acc.astype(BF16).reshape(2, rows, cols)
+
+        @pl.when(side == x)
+        def _():
+            out_send(unit, 1).start()
+            out_own(unit).start()
+
+        @pl.when(side != x)
+        def _():
+            out_send(unit, 2).start()
+            out_send(unit, 3).start()
+
+    def sweep(i, carry):
+        early = i < 2 * planes
+        j = i % planes
+        q = jnp.where(early, j, planes + (i - 2 * planes) // 2)
+        partner = jnp.where(early, i < planes, i % 2 == 0)
+        plane = plane_at(q // 2)
+        other = q % 2
+
+        @pl.when(i == jnp.where(z == 0, planes, 2 * planes))
+        def _():
+            for p in range(1, planes):
+                @pl.when(due[p] >= STEPS)
                 def _():
-                    code_y_in(plane).wait_recv()
-                project(plane * 2 + y + other * (1 - 2 * y))
-
-            return inner
-
-        lax.fori_loop(0, 4, one, 0)
-        return carry
-
-    lax.fori_loop(0, planes, sweep, 0)
+                    relay(p)
+
+        @pl.when(partner & (other == 1))
+        def _():
+            code_y_in(plane).wait_recv()
+
+        @pl.when(i == planes)
+        def _():
+            for t in range(STEPS - LAG, STEPS):
+                rot_x_in(t).wait_recv()
+                rot_f(t).start()
+            lax.fori_loop(STEPS // 2, STEPS, gathered_far, 0)
+        project(plane * 2 + y + other * (1 - 2 * y), jnp.where(partner, 1 - x, x))
+        return carry
+
+    lax.fori_loop(0, 4 * planes, sweep, 0)
 
     for k in (1, 2, 3):
         kv_quad(k).wait_send()

time: 95.9 us -> 82.9 us (0.86)
  Pallas kernels: 89 us -> 76.6 us
    pallas_call x1, Pallas kernels: 89 us -> 76.6 us  [on_device(): pl.pallas_call(functools.partial(kernel, n, reach, slots), out_shape=jax....]
where the time goes in v2:
time: 82.9 us; the launch traced here: 81.7 us
  Pallas kernels  76.6 us (92%)
  local copies, waits for them, and re-layouts  4.38 us (5%)
    pallas_call x1, Pallas kernels, on_device(): pl.pallas_call(functools.partial(kernel, n, reach, slots), out_shape=jax....  76.6 us
    unnamed x3, local copies, waits for them, and re-layouts  3.33 us

profile of v2, /device:TPU:17, one launch (start us, length us, event | category | flops | bytes accessed | tf_op | source)
XLA Modules:
  0.0 81.7 jit_solution(12738616315853024767)
XLA Ops:
  0.0 0.0 copy-start
  0.0 0.7 select_convert_fusion.had_ref
  0.7 0.2 copy-done
  1.0 0.2 bitcast_bitcast_fusion
  1.1 0.9 %reshape.32.kv_ref = bf16[4,128,256]{2,1,0:T(8,128)(2,1)} reshape(bf16[4,128,2,128]{3,2,1,0:T(2,128)(2,1)S(1)} %bitcast_bitcast_fusion) | data formatting | bytes 524288 | tf_op jit(solution)/shard_map/reshape | solution.py:479
  2.0 76.6 %shard_map.55 = bf16[128,8192]{1,0:T(8,128)(2,1)} custom-call(bf16[128,4096]{1,0:T(8,128)(2,1)} %q_ref.1, bf16[4,128,256]{2,1,0:T(8,128)(2,1)} %reshape.32.kv_ref, s32[8,4,128]{2,1,0:T(4,128)} %bitcast.8, bf16[128,128]{1,0:T(8,128)(2,1)} %select_convert_fusion.had_ref, s32[512,256]{1,0:T(8,128)} %codes_ref.1, bf16[32,8192]{1,0:T(8,128)(2,1)} %scales_ref.1), custom_call_target="tpu_custom_call" | custom-call | tf_op jit(solution)/shard_map/pallas_call | solution.py:480
  78.6 3.1 %copy.10 = bf16[128,8192]{1,0:T(8,128)(2,1)} copy(bf16[128,8192]{1,0:T(8,128)(2,1)} %shard_map.55) | data formatting | bytes 4194304
  (1 shorter events, 0.0 us)
Async XLA Ops:
  0.0 1.0 %copy-start = (bf16[128,2,512]{2,1,0:T(2,128)(2,1)S(1)}, bf16[128,2,512]{2,1,0:T(2,128)(2,1)}, u32[]{:S(2)}) copy-start(bf16[128,2,512]{2,1,0:T(2,128)(2,1)} %param.6) | copy-start | bytes 786436

commit v3 on v2

--- a/solution.py
+++ b/solution.py
@@ -38,7 +38,8 @@
 def kernel(
     n, reach, slots,
     q_ref, kv_ref, sign_ref, had_ref, codes_ref, scales_ref, out_ref,
-    win, ones, qbuf, cbuf, rot, bias, stage, local_sem,
+    win, ones, qbuf, cbuf, rot, bias, sbuf, wbuf, stage,
+    q_all, signs_buf, scales, local_sem,
     kq_s, kq_r, qs, qr, zs, zr, ys, yr, up_s, up_r, dn_s, dn_r, cy_s, cy_r,
     rx_s, rx_r, rc_s, rc_r, rf_s, rf_r, os, orr, ol,
 ):
@@ -67,6 +68,17 @@
             device_id={"seq": target}, device_id_type=MESH,
         )
 
+    own_kv = pltpu.make_async_copy(
+        kv_ref.at[lane], win.at[top_slot * QUAD + lane, :, pl.ds(0, 2 * HD)], local_sem.at[0])
+    own_lanes = pl.ds(pl.multiple_of(lane * width, width), width)
+    all_q = pltpu.make_async_copy(q_ref, q_all, local_sem.at[5])
+    own_q = pltpu.make_async_copy(q_ref.at[:, own_lanes], qbuf.at[0], local_sem.at[1])
+    own_codes = pltpu.make_async_copy(codes_ref, cbuf.at[quad], local_sem.at[2])
+    all_signs = pltpu.make_async_copy(sign_ref, signs_buf, local_sem.at[3])
+    all_scales = pltpu.make_async_copy(scales_ref, scales, local_sem.at[4])
+    for copy in (own_kv, all_q, own_codes, own_q, all_signs, all_scales):
+        copy.start()
+
     barrier = pltpu.get_barrier_semaphore()
 
     def greet(target):
@@ -84,15 +96,6 @@
     def _():
         greet(down)
 
-    own_kv = pltpu.make_async_copy(
-        kv_ref.at[lane], win.at[top_slot * QUAD + lane, :, pl.ds(0, 2 * HD)], local_sem.at[0])
-    own_lanes = pl.ds(pl.multiple_of(lane * width, width), width)
-    own_q = pltpu.make_async_copy(q_ref.at[:, own_lanes], qbuf.at[0], local_sem.at[1])
-    own_codes = pltpu.make_async_copy(codes_ref, cbuf.at[quad], local_sem.at[2])
-    own_kv.start()
-    own_q.start()
-    own_codes.start()
-
     pl.semaphore_wait(barrier, QUAD + has_up.astype(jnp.int32) + has_down.astype(jnp.int32))
 
     def block(slot, k):
@@ -135,19 +138,19 @@
 
     def q_quad(k):
         lanes = pl.ds(pl.multiple_of((lane + off(k)) * width, width), width)
-        return remote(q_ref.at[:, lanes], qbuf.at[k], qs.at[k], qr.at[k], me + off(k))
+        return remote(q_all.at[:, lanes], qbuf.at[k], qs.at[k], qr.at[k], me + off(k))
 
     def code_up(k):
-        unit = cbuf.at[quad - 2 * k] if not isinstance(k, int) or k > 0 else codes_ref
-        return remote(unit, cbuf.at[quad - 2 * k], up_s.at[k + 1], up_r.at[k + 1], up)
+        unit = cbuf.at[quad - 2 * k]
+        return remote(unit, unit, up_s.at[k + 1], up_r.at[k + 1], up)
 
     def code_up_in(k):
         unit = cbuf.at[quad - 2 * k]
         return remote(unit, unit, up_s.at[k], up_r.at[k], up)
 
     def code_down(k):
-        unit = cbuf.at[quad + 2 * k] if not isinstance(k, int) or k > 0 else codes_ref
-        return remote(unit, cbuf.at[quad + 2 * k], dn_s.at[k + 1], dn_r.at[k + 1], down)
+        unit = cbuf.at[quad + 2 * k]
+        return remote(unit, unit, dn_s.at[k + 1], dn_r.at[k + 1], down)
 
     def code_down_in(k):
         unit = cbuf.at[quad + 2 * k]
@@ -168,14 +171,18 @@
         both = z + ((p + 1) // 2) * (2 * (p % 2) - 1)
         return jnp.where(p <= 2 * near, both, z + toward * (p - near))
 
-    begin = jnp.where(z == 0, 125, jnp.where(z == 1, 186, jnp.where(z == 2, 220, 200)))
-    due = [None]
+    begin = jnp.where(z == 0, 80, jnp.where(z == 1, 138, 175))
+    due, item_due = [None], [None]
+    early = planes + 1
     for p in range(1, planes):
         d = plane_at(p) - z
-        arrival = jnp.where(d > 0, 53 + 130 * d, jnp.where(z == 1, 123, 183) - 117 * d)
-        step = jnp.maximum((arrival - begin - 17) // 33, 0)
-        step = jnp.where((d == 1) & has_down, -1, step)
-        due.append(step if p == 1 else jnp.maximum(due[-1], step))
+        arrival = jnp.where(d > 0, 130 * d, jnp.where(z == 1, 71, 130) - 117 * d)
+        step_due = jnp.maximum((arrival - begin - 10) // 20, 0)
+        step_due = jnp.where((d == 1) & has_down, -1, step_due)
+        due.append(step_due if p == 1 else jnp.maximum(due[-1], step_due))
+        first_use = 2 * p - 1 if 2 * p - 1 < early else 2 * early + 2 * (2 * p - 1 - early)
+        item = jnp.minimum(jnp.maximum(arrival - begin - 19 * STEPS - 10, 0) // 9, first_use)
+        item_due.append(item if p == 1 else jnp.maximum(item_due[-1], item))
 
     def relay(p):
         plane = plane_at(p)
@@ -202,18 +209,22 @@
         kv_quad(k).start()
     forward_kv(top_slot, 0, lambda copy: copy.start())
 
+    own_codes.wait()
+
     @pl.when(has_down)
     def _():
         code_down(0).start()
+    all_q.wait()
     for k in (1, 2, 3):
         q_quad(k).start()
 
     window_blocks = reach + 1
     keys = window_blocks * rows
-    query = lax.broadcasted_iota(jnp.int32, (rows, keys), 0)
-    key = lax.broadcasted_iota(jnp.int32, (rows, keys), 1) - reach * rows
-    gap = query - key
-    bias[...] = jnp.where((gap >= 0) & (gap < WINDOW), 0.0, -jnp.inf).astype(F32)
+    for edge, offset in ((0, reach * rows), (1, 0)):
+        query = lax.broadcasted_iota(jnp.int32, (rows, rows), 0)
+        key = lax.broadcasted_iota(jnp.int32, (rows, rows), 1) - offset
+        gap = query - key
+        bias[:, edge * rows:(edge + 1) * rows] = jnp.where((gap >= 0) & (gap < WINDOW), 0.0, -jnp.inf).astype(F32)
     for slot in range(slots):
         value = jnp.where(there(slot), 1.0, 0.0).astype(F32)
         ones[slot * QUAD:(slot + 1) * QUAD] = jnp.full((QUAD, rows, HD), value, F32).astype(BF16)
@@ -230,8 +241,6 @@
             forward_kv(slot, k, lambda copy: copy.start())
         if slot in (top_slot - 2, 0):
             if slot == top_slot - 2:
-                own_codes.wait()
-
                 @pl.when(has_up)
                 def _():
                     code_up(0).start()
@@ -261,6 +270,8 @@
                 level = (top_slot - 1 - slot) // 2
                 remote(block(slot, k), block(slot, k), ys.at[level, k], yr.at[level, k], me + dy).wait_recv()
     own_q.wait()
+    all_signs.wait()
+    all_scales.wait()
 
     def piece(r, source_lane, half):
         start = source_lane * width + half * half_width
@@ -294,29 +305,43 @@
         ref = piece(lane + dc + dx - (k % 2) * dc - (k // 2) * dx, lane + dc + dx, t % 2)
         return remote(ref, ref, rf_s.at[t], rf_r.at[t], me + dc)
 
-    def attend(t, carry):
+    first_edge, last_edge = rows, keys - rows
+
+    def score(t, slot):
         k = t // HALVES
         half = t % HALVES
-        r = lane + off(k)
-
-        @pl.when((half == 0) & (k > 0))
-        def _():
-            remote(qbuf.at[k], qbuf.at[k], qs.at[k], qr.at[k], me + off(k)).wait_recv()
-
         lanes = pl.ds(pl.multiple_of(half * half_width, half_width), half_width)
         q = qbuf[k, :, lanes]
         q = jnp.concatenate([q[:, h * HD:(h + 1) * HD] for h in range(PER_STEP)], axis=0)
-        k_rows = win[pl.ds(r, window_blocks), :, 0:HD].reshape(keys, HD)
+        scaled = q.astype(F32) * (LOG2E / math.sqrt(HD))
+        high = scaled.astype(BF16)
+        low = (scaled - high.astype(F32)).astype(BF16)
+        q = jnp.concatenate([high, low], axis=1)
+        k_rows = win[pl.ds(lane + off(k), window_blocks), :, 0:HD].reshape(keys, HD)
+        k_rows = jnp.concatenate([k_rows, k_rows], axis=1)
+        sbuf[slot] = lax.dot_general(q, k_rows, (((1,), (1,)), ((), ())), preferred_element_type=F32)
+
+    def soften(t, slot):
+        r = lane + off(t // HALVES)
+        scores = sbuf[slot].reshape(PER_STEP, rows, keys)
+        scores = jnp.concatenate([
+            scores[:, :, :first_edge] + bias[:, :rows][None],
+            scores[:, :, first_edge:last_edge],
+            scores[:, :, last_edge:] + bias[:, rows:][None],
+        ], axis=2)
+        top = jnp.max(scores, axis=-1, keepdims=True)
+        weights = jnp.exp2(scores - top).astype(BF16)
         v_rows = win[pl.ds(r, window_blocks), :, HD:2 * HD].reshape(keys, HD)
         v_rows = jnp.concatenate([v_rows, ones[pl.ds(r, window_blocks)].reshape(keys, HD)], axis=1)
-        scores = lax.dot_general(q, k_rows, (((1,), (1,)), ((), ())), preferred_element_type=F32)
-        scores = scores.reshape(PER_STEP, rows, keys) * (LOG2E / math.sqrt(HD)) + bias[...][None]
-        top = jnp.max(scores, axis=-1, keepdims=True)
-        weights = jnp.exp2(scores - top).astype(BF16)
         weighted = jnp.dot(weights.reshape(PER_STEP * rows, keys), v_rows, preferred_element_type=F32)
         weighted = weighted[:, :HD] / weighted[:, HD:]
-        signs = sign_ref[lane * HALVES + half].astype(F32)
-        signed = weighted.reshape(PER_STEP, rows, HD) * signs[:, None, :]
+        wbuf[...] = weighted
+
+    def rotate(t):
+        k = t // HALVES
+        half = t % HALVES
+        signs = signs_buf[lane * HALVES + half].astype(F32)
+        signed = wbuf[...].reshape(PER_STEP, rows, HD) * signs[:, None, :]
         signed = signed.reshape(PER_STEP * rows, HD)
         high = signed.astype(BF16)
         low = (signed - high.astype(F32)).astype(BF16)
@@ -325,7 +350,15 @@
         mixed = (mixed * (1.0 / math.sqrt(HD))).astype(BF16)
         start = lane * width + half * half_width
         for h in range(PER_STEP):
-            rot[r, :, pl.ds(pl.multiple_of(start + h * HD, HD), HD)] = mixed[h * rows:(h + 1) * rows]
+            rot[lane + off(k), :, pl.ds(pl.multiple_of(start + h * HD, HD), HD)] = mixed[h * rows:(h + 1) * rows]
+
+    def step(t, slot):
+        score(jnp.minimum(t + 1, STEPS - 1), 1 - slot)
+        soften(t, slot)
+
+        @pl.when(me < n)
+        def _():
+            rotate(t)
 
         @pl.when(t >= LAG)
         def _():
@@ -339,9 +372,18 @@
 
         rot_x(t).start()
         rot_c(t).start()
-        return carry
-
-    lax.fori_loop(0, STEPS, attend, 0)
+
+    def attend(k, carry):
+        step(k * HALVES, 0)
+
+        @pl.when(k < QUAD - 1)
+        def _():
+            remote(qbuf.at[k + 1], qbuf.at[k + 1], qs.at[k + 1], qr.at[k + 1], me + off(k + 1)).wait_recv()
+        step(k * HALVES + 1, 1)
+        return carry
+
+    score(0, 0)
+    lax.fori_loop(0, QUAD, attend, 0)
     def gathered(t, carry):
         rot_c_in(t).wait_recv()
         return carry
@@ -371,7 +413,7 @@
         return pltpu.make_async_copy(stage.at[unit, lane], out_ref.at[:, lanes_of(unit, lane)], ol.at[unit])
 
     def project(unit, side):
-        scale = scales_ref[:, lanes_of(unit, lane)]
+        scale = scales[:, lanes_of(unit, lane)]
         acc = jnp.zeros((2 * rows, cols), F32)
         for chunk in range(HEADS // chunk_heads):
             parts = []
@@ -398,30 +440,29 @@
             out_send(unit, 3).start()
 
     def sweep(i, carry):
-        early = i < 2 * planes
-        j = i % planes
-        q = jnp.where(early, j, planes + (i - 2 * planes) // 2)
-        partner = jnp.where(early, i < planes, i % 2 == 0)
+        first = i < 2 * early
+        rest = i - 2 * early
+        q = jnp.where(first, i % early, early + rest // 2)
+        partner = jnp.where(first, i < early, rest % 2 == 0)
         plane = plane_at(q // 2)
         other = q % 2
 
-        @pl.when(i == jnp.where(z == 0, planes, 2 * planes))
-        def _():
-            for p in range(1, planes):
-                @pl.when(due[p] >= STEPS)
-                def _():
-                    relay(p)
-
-        @pl.when(partner & (other == 1))
-        def _():
-            code_y_in(plane).wait_recv()
-
-        @pl.when(i == planes)
+        for p in range(1, planes):
+            @pl.when((i == item_due[p]) & (due[p] >= STEPS))
+            def _():
+                relay(p)
+
+        @pl.when(i == early)
         def _():
             for t in range(STEPS - LAG, STEPS):
                 rot_x_in(t).wait_recv()
                 rot_f(t).start()
             lax.fori_loop(STEPS // 2, STEPS, gathered_far, 0)
+
+        @pl.when(partner & (other == 1))
+        def _():
+            code_y_in(plane).wait_recv()
+
         project(plane * 2 + y + other * (1 - 2 * y), jnp.where(partner, 1 - x, x))
         return carry
 
@@ -475,12 +516,14 @@
     planes = n // (2 * QUAD)
     word_rows, cols = out_codes.shape
     vmem = pl.BlockSpec(memory_space=pltpu.VMEM)
+    hbm = pl.BlockSpec(memory_space=pltpu.HBM)
+    in_hbm = functools.partial(pltpu.with_memory_space_constraint, memory_space=pltpu.HBM)
     dma = pltpu.SemaphoreType.DMA
     per_head = keys_values.reshape(rows, 2, KV, HD).transpose(2, 0, 1, 3).reshape(KV, rows, 2 * HD)
     return pl.pallas_call(
         functools.partial(kernel, n, reach, slots),
-        out_shape=jax.ShapeDtypeStruct((rows, n * cols), BF16),
-        in_specs=[vmem] * 6,
+        out_shape=pltpu.VMEM((rows, n * cols), BF16),
+        in_specs=[hbm, vmem, hbm, vmem, hbm, hbm],
         out_specs=pl.BlockSpec(memory_space=pl.ANY),
         scratch_shapes=[
             pltpu.VMEM((slots * QUAD, rows, 2 * HD), BF16),
@@ -488,9 +531,14 @@
             pltpu.VMEM((QUAD, rows, LANE_HEADS * HD), BF16),
             pltpu.VMEM((2 * planes, word_rows, cols), jnp.int32),
             pltpu.VMEM((QUAD, rows, HEADS * HD), BF16),
-            pltpu.VMEM((rows, (reach + 1) * rows), F32),
+            pltpu.VMEM((rows, 2 * rows), F32),
+            pltpu.VMEM((2, PER_STEP * rows, (reach + 1) * rows), F32),
+            pltpu.VMEM((PER_STEP * rows, HD), F32),
             pltpu.VMEM((2 * planes, QUAD, rows, cols), BF16),
-            dma((3,)),
+            pltpu.VMEM((rows, HEADS * HD), BF16),
+            pltpu.VMEM((STEPS, PER_STEP, HD), jnp.int32),
+            pltpu.VMEM((HEADS, n * cols), BF16),
+            dma((6,)),
             dma((QUAD,)), dma((QUAD,)),
             dma((QUAD,)), dma((QUAD,)),
             dma((slots // 2, QUAD)), dma((slots // 2, QUAD)),
@@ -505,15 +553,15 @@
             dma((2 * planes,)),
         ],
         compiler_params=pltpu.CompilerParams(
-            collective_id=0, has_side_effects=True, vmem_limit_bytes=64 * 1000 * 1000
+            collective_id=0, has_side_effects=True, vmem_limit_bytes=52 * 1000 * 1000
         ),
     )(
-        queries,
+        in_hbm(queries),
         per_head,
-        head_signs.reshape(STEPS, PER_STEP, HD),
+        in_hbm(head_signs.reshape(STEPS, PER_STEP, HD)),
         reordered_hadamard(),
-        out_codes,
-        out_scales,
+        in_hbm(out_codes),
+        in_hbm(out_scales),
     )
 
 

time: 82.9 us -> 78.8 us (0.951)
  the two profiles are of different devices: /device:TPU:17 before, /device:TPU:29 now
where the time goes in v3:
time: 78.8 us; the launch traced here: 78.6 us
  Pallas kernels  76 us (96%)
  local copies, waits for them, and re-layouts  2.52 us (3%)
    pallas_call x1, Pallas kernels, on_device(): pl.pallas_call(functools.partial(kernel, n, reach, slots), out_shape=pltp...  76 us
    unnamed x3, local copies, waits for them, and re-layouts  2.17 us

profile of v3, /device:TPU:29, one launch (start us, length us, event | category | flops | bytes accessed | tf_op | source)
XLA Modules:
  0.0 78.6 jit_solution(14755869055166421161)
XLA Ops:
  0.0 0.0 copy-start
  0.0 0.1 select_convert_fusion.had_ref
  0.1 0.8 %copy-done = bf16[128,2,512]{2,1,0:T(2,128)(2,1)S(1)} copy-done((bf16[128,2,512]{2,1,0:T(2,128)(2,1)S(1)}, bf16[128,2,512]{2,1,0:T(2,128)(2,1)}, u32[]{:S(2)}) %copy-start) | copy-done | bytes 262168
  1.0 0.2 bitcast_bitcast_fusion
  1.1 0.2 reshape.32.kv_ref
  1.3 76.0 %shard_map.55 = bf16[128,8192]{1,0:T(8,128)(2,1)S(1)} custom-call(bf16[128,4096]{1,0:T(8,128)(2,1)} %q_ref.1, bf16[4,128,256]{2,1,0:T(8,128)(2,1)S(1)} %reshape.32.kv_ref, s32[8,4,128]{2,1,0:T(4,128)} %bitcast.8, bf16[128,128]{1,0:T(8,128)(2,1)S(1)} %select_convert_fusion.had_ref, s32[512,256]{1,0:T(8,128)} %codes_ref.1, bf16[32,8192]{1,0:T(8,128)(2,1)} %scales_ref.1), custom_call_target="tpu_custom_call" | custom-call | tf_op jit(solution)/shard_map/pallas_call | solution.py:523
  77.3 1.3 %copy.10 = bf16[128,8192]{1,0:T(8,128)(2,1)} copy(bf16[128,8192]{1,0:T(8,128)(2,1)S(1)} %shard_map.55) | data formatting | bytes 4194304
  (1 shorter events, 0.0 us)
Async XLA Ops:
  0.0 1.0 %copy-start = (bf16[128,2,512]{2,1,0:T(2,128)(2,1)S(1)}, bf16[128,2,512]{2,1,0:T(2,128)(2,1)}, u32[]{:S(2)}) copy-start(bf16[128,2,512]{2,1,0:T(2,128)(2,1)} %param.6) | copy-start | bytes 786436

commit v4 on v3

--- a/solution.py
+++ b/solution.py
@@ -18,7 +18,7 @@
 HALVES = 2
 PER_STEP = LANE_HEADS // HALVES
 STEPS = QUAD * HALVES
-LAG = 3
+LAG = 5
 LOG2E = 1.4426950408889634
 MESH = pl.DeviceIdType.MESH
 BF16 = jnp.bfloat16
@@ -40,7 +40,7 @@
     q_ref, kv_ref, sign_ref, had_ref, codes_ref, scales_ref, out_ref,
     win, ones, qbuf, cbuf, rot, bias, sbuf, wbuf, stage,
     q_all, signs_buf, scales, local_sem,
-    kq_s, kq_r, qs, qr, zs, zr, ys, yr, up_s, up_r, dn_s, dn_r, cy_s, cy_r,
+    kq_s, kq_r, qs, qr, zs, zr, ys, yr, up_s, up_r, dn_s, dn_r, cy_s, cy_r, cross_s, cross_r,
     rx_s, rx_r, rc_s, rc_r, rf_s, rf_r, os, orr, ol,
 ):
     rows = q_ref.shape[0]
@@ -156,13 +156,36 @@
         unit = cbuf.at[quad + 2 * k]
         return remote(unit, unit, dn_s.at[k], dn_r.at[k], down)
 
-    def code_y(plane):
-        unit = cbuf.at[plane * 2 + y]
-        return remote(unit, unit, cy_s.at[plane], cy_r.at[plane], me + dy)
-
-    def code_y_in(plane):
-        unit = cbuf.at[plane * 2 + 1 - y]
-        return remote(unit, unit, cy_s.at[plane], cy_r.at[plane], me + dy)
+    half_words = cbuf.shape[1] // 2
+
+    def far(plane):
+        return ((plane == 0) | (plane == planes - 1)) & (plane != z)
+
+    def each_y(plane, column, act):
+        def copy(unit):
+            return remote(unit, unit, cy_s.at[plane], cy_r.at[plane], me + dy)
+
+        @pl.when(far(plane))
+        def _():
+            act(copy(cbuf.at[plane * 2 + column, pl.ds(0, half_words)]))
+
+        @pl.when(jnp.logical_not(far(plane)))
+        def _():
+            act(copy(cbuf.at[plane * 2 + column]))
+
+    def send_y(plane):
+        each_y(plane, y, lambda copy: copy.start())
+
+    def wait_y(plane):
+        each_y(plane, 1 - y, lambda copy: copy.wait_recv())
+
+    def cross_up():
+        unit = cbuf.at[1 - y, pl.ds(half_words, half_words)]
+        return remote(unit, unit, cross_s.at[0], cross_r.at[0], up)
+
+    def cross_down():
+        unit = cbuf.at[(planes - 1) * 2 + 1 - y, pl.ds(half_words, half_words)]
+        return remote(unit, unit, cross_s.at[1], cross_r.at[1], down)
 
     near = jnp.minimum(z, planes - 1 - z)
     toward = jnp.where(z <= planes - 1 - z, 1, -1)
@@ -171,39 +194,94 @@
         both = z + ((p + 1) // 2) * (2 * (p % 2) - 1)
         return jnp.where(p <= 2 * near, both, z + toward * (p - near))
 
-    begin = jnp.where(z == 0, 80, jnp.where(z == 1, 138, 175))
-    due, item_due = [None], [None]
     early = planes + 1
+
+    def relay(p):
+        plane = plane_at(p)
+
+        @pl.when(plane < z)
+        def _():
+            code_up_in(z - plane).wait_recv()
+
+            @pl.when(has_up)
+            def _():
+                code_up(z - plane).start()
+            send_y(plane)
+
+        @pl.when(plane > z)
+        def _():
+            code_down_in(plane - z).wait_recv()
+
+            @pl.when(has_down)
+            def _():
+                code_down(plane - z).start()
+            send_y(plane)
+
+    def own_y():
+        wait_y(z)
+
+        @pl.when((z == 0) & has_up)
+        def _():
+            cross_up().start()
+
+        @pl.when((z == planes - 1) & has_down)
+        def _():
+            cross_down().start()
+
+    def relay_cross_up():
+        @pl.when(has_down)
+        def _():
+            cross_up().wait_recv()
+
+            @pl.when(has_up)
+            def _():
+                cross_up().start()
+
+    def relay_cross_down():
+        @pl.when(has_up)
+        def _():
+            cross_down().wait_recv()
+
+            @pl.when(has_down)
+            def _():
+                cross_down().start()
+
+    begin = jnp.where(z == 0, 80, jnp.where(z == 1, 138, 165))
+    after = begin + 19 * STEPS + 15
+
+    def item_of(q):
+        return STEPS + jnp.where(q < early, q, 2 * early + 2 * (q - early))
+
+    events = []
+
+    def expect(action, arrival, deadline, prologue=None):
+        step_at = jnp.clip((arrival - begin - 10) // 20, 0, STEPS - 1)
+        item_at = STEPS + jnp.maximum(arrival - after, 0) // 9
+        at = jnp.minimum(jnp.where(arrival < after, step_at, item_at), deadline)
+        if prologue is not None:
+            at = jnp.where(prologue, -1, at)
+        events.append((action, arrival, at))
+
     for p in range(1, planes):
         d = plane_at(p) - z
         arrival = jnp.where(d > 0, 130 * d, jnp.where(z == 1, 71, 130) - 117 * d)
-        step_due = jnp.maximum((arrival - begin - 10) // 20, 0)
-        step_due = jnp.where((d == 1) & has_down, -1, step_due)
-        due.append(step_due if p == 1 else jnp.maximum(due[-1], step_due))
-        first_use = 2 * p - 1 if 2 * p - 1 < early else 2 * early + 2 * (2 * p - 1 - early)
-        item = jnp.minimum(jnp.maximum(arrival - begin - 19 * STEPS - 10, 0) // 9, first_use)
-        item_due.append(item if p == 1 else jnp.maximum(item_due[-1], item))
-
-    def relay(p):
-        plane = plane_at(p)
-
-        @pl.when(plane < z)
-        def _():
-            code_up_in(z - plane).wait_recv()
-
-            @pl.when(has_up)
-            def _():
-                code_up(z - plane).start()
-            code_y(plane).start()
-
-        @pl.when(plane > z)
-        def _():
-            code_down_in(plane - z).wait_recv()
-
-            @pl.when(has_down)
-            def _():
-                code_down(plane - z).start()
-            code_y(plane).start()
+        expect(functools.partial(relay, p), arrival, item_of(2 * p - 1), (d == 1) & has_down)
+    expect(own_y, jnp.where(z == 0, 185, jnp.where(z == 1, 255, 290)), item_of(1))
+    bottom = jnp.where(z == near, 2 * z, planes - 1)
+    top_at = jnp.where(planes - 1 - z == near, 2 * near - 1, planes - 1)
+    expect(relay_cross_up, jnp.where(z == 1, 275, 170 + 130 * z), item_of(2 * bottom + 1))
+    expect(relay_cross_down, 290 + 71 * (planes - 1 - z), item_of(2 * jnp.maximum(top_at, 0) + 1))
+    timed = []
+    for action, arrival, _ in events:
+        at = None
+        for _, other_arrival, other_at in events:
+            later = jnp.where(other_arrival >= arrival, other_at, STEPS + 4 * planes)
+            at = later if at is None else jnp.minimum(at, later)
+        timed.append((action, at))
+
+    def run_events(now):
+        for action, at in timed:
+            pl.when(at == now)(action)
 
     for k in (2, 3, 1):
         kv_quad(k).start()
@@ -229,31 +307,45 @@
         value = jnp.where(there(slot), 1.0, 0.0).astype(F32)
         ones[slot * QUAD:(slot + 1) * QUAD] = jnp.full((QUAD, rows, HD), value, F32).astype(BF16)
 
-    for k in (1, 2, 3):
+    def take_quad(k):
         kv_quad_in(k).wait_recv()
         forward_kv(top_slot, k, lambda copy: copy.start())
+
+    def take_z(slot, k):
+        @pl.when(there(slot))
+        def _():
+            z_kv(slot + 2, k).wait_recv()
+        forward_kv(slot, k, lambda copy: copy.start())
+
+    levels = range(top_slot - 2, -1, -2)
+    take_quad(1)
     own_kv.wait()
-    for slot in range(top_slot - 2, -1, -2):
-        for k in range(QUAD):
-            @pl.when(there(slot))
-            def _():
-                z_kv(slot + 2, k).wait_recv()
-            forward_kv(slot, k, lambda copy: copy.start())
-        if slot in (top_slot - 2, 0):
-            if slot == top_slot - 2:
-                @pl.when(has_up)
-                def _():
-                    code_up(0).start()
-
-            @pl.when(y == (0 if slot == top_slot - 2 else 1))
-            def _():
-                code_y(z).start()
-
-    for p in range(1, planes):
-        @pl.when(due[p] < 0)
-        def _():
-            relay(p)
-
+    take_z(top_slot - 2, 0)
+    take_z(top_slot - 2, 1)
+    take_quad(2)
+    take_quad(3)
+    for slot in levels[1:]:
+        take_z(slot, 0)
+        take_z(slot, 1)
+    take_z(top_slot - 2, 2)
+    take_z(top_slot - 2, 3)
+
+    @pl.when(has_up)
+    def _():
+        code_up(0).start()
+
+    @pl.when(y == 0)
+    def _():
+        send_y(z)
+    for slot in levels[1:]:
+        take_z(slot, 2)
+        take_z(slot, 3)
+
+    @pl.when(y == 1)
+    def _():
+        send_y(z)
+
+    run_events(-1)
     for slot in range(top_slot):
         @pl.when(jnp.logical_not(there(slot)))
         def _():
@@ -365,11 +457,7 @@
             rot_x_in(t - LAG).wait_recv()
             rot_f(t - LAG).start()
 
-        for p in range(1, planes):
-            @pl.when(t == due[p])
-            def _():
-                relay(p)
-
+        run_events(t)
         rot_x(t).start()
         rot_c(t).start()
 
@@ -384,6 +472,10 @@
 
     score(0, 0)
     lax.fori_loop(0, QUAD, attend, 0)
+    for t in range(STEPS - LAG, STEPS // 2):
+        rot_x_in(t).wait_recv()
+        rot_f(t).start()
+
     def gathered(t, carry):
         rot_c_in(t).wait_recv()
         return carry
@@ -447,21 +539,18 @@
         plane = plane_at(q // 2)
         other = q % 2
 
-        for p in range(1, planes):
-            @pl.when((i == item_due[p]) & (due[p] >= STEPS))
-            def _():
-                relay(p)
+        run_events(STEPS + i)
 
         @pl.when(i == early)
         def _():
-            for t in range(STEPS - LAG, STEPS):
+            for t in range(max(STEPS - LAG, STEPS // 2), STEPS):
                 rot_x_in(t).wait_recv()
                 rot_f(t).start()
             lax.fori_loop(STEPS // 2, STEPS, gathered_far, 0)
 
-        @pl.when(partner & (other == 1))
-        def _():
-            code_y_in(plane).wait_recv()
+        @pl.when(partner & (other == 1) & (plane != z))
+        def _():
+            wait_y(plane)
 
         project(plane * 2 + y + other * (1 - 2 * y), jnp.where(partner, 1 - x, x))
         return carry
@@ -483,10 +572,18 @@
         @pl.when((z + k < planes) & has_down)
         def _():
             code_down(k).wait_send()
-        code_y(k).wait_send()
+        each_y(k, y, lambda copy: copy.wait_send())
         return carry
 
     lax.fori_loop(0, planes, drain_codes, 0)
+
+    @pl.when(has_up)
+    def _():
+        cross_up().wait_send()
+
+    @pl.when(has_down)
+    def _():
+        cross_down().wait_send()
 
     def drain_rot(t, carry):
         rot_x(t).wait_send()
@@ -546,6 +643,7 @@
             dma((planes + 1,)), dma((planes + 1,)),
             dma((planes + 1,)), dma((planes + 1,)),
             dma((planes,)), dma((planes,)),
+            dma((2,)), dma((2,)),
             dma((STEPS,)), dma((STEPS,)),
             dma((STEPS,)), dma((STEPS,)),
             dma((STEPS,)), dma((STEPS,)),

time: 78.8 us -> 72.4 us (0.919)
  the two profiles are of different devices: /device:TPU:29 before, /device:TPU:17 now
where the time goes in v4:
time: 72.4 us; the launch traced here: 71.9 us
  Pallas kernels  69.3 us (96%)
  local copies, waits for them, and re-layouts  2.52 us (3%)
    pallas_call x1, Pallas kernels, on_device(): pl.pallas_call(functools.partial(kernel, n, reach, slots), out_shape=pltp...  69.3 us
    unnamed x3, local copies, waits for them, and re-layouts  2.17 us

profile of v4, /device:TPU:17, one launch (start us, length us, event | category | flops | bytes accessed | tf_op | source)
XLA Modules:
  0.0 71.9 jit_solution(6253122894944905202)
XLA Ops:
  0.0 0.0 copy-start
  0.0 0.1 select_convert_fusion.had_ref
  0.1 0.8 %copy-done = bf16[128,2,512]{2,1,0:T(2,128)(2,1)S(1)} copy-done((bf16[128,2,512]{2,1,0:T(2,128)(2,1)S(1)}, bf16[128,2,512]{2,1,0:T(2,128)(2,1)}, u32[]{:S(2)}) %copy-start) | copy-done | bytes 262168
  1.0 0.2 bitcast_bitcast_fusion
  1.1 0.2 reshape.32.kv_ref
  1.3 69.3 %shard_map.55 = bf16[128,8192]{1,0:T(8,128)(2,1)S(1)} custom-call(bf16[128,4096]{1,0:T(8,128)(2,1)} %q_ref.1, bf16[4,128,256]{2,1,0:T(8,128)(2,1)S(1)} %reshape.32.kv_ref, s32[8,4,128]{2,1,0:T(4,128)} %bitcast.8, bf16[128,128]{1,0:T(8,128)(2,1)S(1)} %select_convert_fusion.had_ref, s32[512,256]{1,0:T(8,128)} %codes_ref.1, bf16[32,8192]{1,0:T(8,128)(2,1)} %scales_ref.1), custom_call_target="tpu_custom_call" | custom-call | tf_op jit(solution)/shard_map/pallas_call | solution.py:620
  70.6 1.3 %copy.10 = bf16[128,8192]{1,0:T(8,128)(2,1)} copy(bf16[128,8192]{1,0:T(8,128)(2,1)S(1)} %shard_map.55) | data formatting | bytes 4194304
  (1 shorter events, 0.0 us)
Async XLA Ops:
  0.0 1.0 %copy-start = (bf16[128,2,512]{2,1,0:T(2,128)(2,1)S(1)}, bf16[128,2,512]{2,1,0:T(2,128)(2,1)}, u32[]{:S(2)}) copy-start(bf16[128,2,512]{2,1,0:T(2,128)(2,1)} %param.6) | copy-start | bytes 786436

commit v5 on v4

--- a/solution.py
+++ b/solution.py
@@ -38,8 +38,8 @@
 def kernel(
     n, reach, slots,
     q_ref, kv_ref, sign_ref, had_ref, codes_ref, scales_ref, out_ref,
-    win, ones, qbuf, cbuf, rot, bias, sbuf, wbuf, stage,
-    q_all, signs_buf, scales, local_sem,
+    win, ones, qbuf, cbuf, rot, bias, sbuf, wbuf, tops, sums, stage,
+    q_all, signs_buf, scales, kv_raw, kv_heads, local_sem,
     kq_s, kq_r, qs, qr, zs, zr, ys, yr, up_s, up_r, dn_s, dn_r, cy_s, cy_r, cross_s, cross_r,
     rx_s, rx_r, rc_s, rc_r, rf_s, rf_r, os, orr, ol,
 ):
@@ -68,15 +68,18 @@
             device_id={"seq": target}, device_id_type=MESH,
         )
 
+    window_blocks = reach + 1
+    keys = window_blocks * rows
+    raw_kv = pltpu.make_async_copy(kv_ref, kv_raw, local_sem.at[6])
     own_kv = pltpu.make_async_copy(
-        kv_ref.at[lane], win.at[top_slot * QUAD + lane, :, pl.ds(0, 2 * HD)], local_sem.at[0])
+        kv_heads.at[lane], win.at[top_slot * QUAD + lane, :, pl.ds(0, 2 * HD)], local_sem.at[0])
     own_lanes = pl.ds(pl.multiple_of(lane * width, width), width)
     all_q = pltpu.make_async_copy(q_ref, q_all, local_sem.at[5])
     own_q = pltpu.make_async_copy(q_ref.at[:, own_lanes], qbuf.at[0], local_sem.at[1])
     own_codes = pltpu.make_async_copy(codes_ref, cbuf.at[quad], local_sem.at[2])
     all_signs = pltpu.make_async_copy(sign_ref, signs_buf, local_sem.at[3])
     all_scales = pltpu.make_async_copy(scales_ref, scales, local_sem.at[4])
-    for copy in (own_kv, all_q, own_codes, own_q, all_signs, all_scales):
+    for copy in (raw_kv, all_q, own_codes, own_q, all_signs, all_scales):
         copy.start()
 
     barrier = pltpu.get_barrier_semaphore()
@@ -96,20 +99,30 @@
     def _():
         greet(down)
 
+    raw_kv.wait()
+    pairs = kv_raw[...].reshape(2 * rows, KV * HD)
+    to = lax.broadcasted_iota(jnp.int32, (rows, 2 * rows), 0)
+    source_row = lax.broadcasted_iota(jnp.int32, (rows, 2 * rows), 1)
+    for which in range(2):
+        pick = jnp.where(source_row == 2 * to + which, 1.0, 0.0).astype(BF16)
+        picked = jnp.dot(pick, pairs, preferred_element_type=F32).astype(BF16)
+        for g in range(KV):
+            kv_heads[g, :, which * HD:(which + 1) * HD] = picked[:, g * HD:(g + 1) * HD]
     pl.semaphore_wait(barrier, QUAD + has_up.astype(jnp.int32) + has_down.astype(jnp.int32))
 
+    own_kv.start()
     def block(slot, k):
         return win.at[slot * QUAD + lane + off(k), :, pl.ds(0, 2 * HD)]
 
     def kv_quad(k):
-        return remote(kv_ref.at[lane + off(k)], win.at[top_slot * QUAD + lane, :, pl.ds(0, 2 * HD)],
+        return remote(kv_heads.at[lane + off(k)], win.at[top_slot * QUAD + lane, :, pl.ds(0, 2 * HD)],
                       kq_s.at[k], kq_r.at[k], me + off(k))
 
     def kv_quad_in(k):
         return remote(block(top_slot, k), block(top_slot, k), kq_s.at[k], kq_r.at[k], me + off(k))
 
     def source(slot, k):
-        return kv_ref.at[lane] if slot == top_slot and k == 0 else block(slot, k)
+        return kv_heads.at[lane] if slot == top_slot and k == 0 else block(slot, k)
 
     def z_kv(slot, k):
         return remote(source(slot, k), block(slot - 2, k),
@@ -247,7 +260,8 @@
                 cross_down().start()
 
     begin = jnp.where(z == 0, 80, jnp.where(z == 1, 138, 165))
-    after = begin + 19 * STEPS + 15
+    after = jnp.where(z == 0, 295, jnp.where(z == 1, 318, 335))
+    stall = 55
 
     def item_of(q):
         return STEPS + jnp.where(q < early, q, 2 * early + 2 * (q - early))
@@ -256,7 +270,9 @@
 
     def expect(action, arrival, deadline, prologue=None):
         step_at = jnp.clip((arrival - begin - 10) // 20, 0, STEPS - 1)
-        item_at = STEPS + jnp.maximum(arrival - after, 0) // 9
+        wait = arrival - after
+        later = early + jnp.maximum(wait - 9 * early - stall, 0) // 9
+        item_at = STEPS + jnp.where(wait < 9 * early, wait // 9, later)
         at = jnp.minimum(jnp.where(arrival < after, step_at, item_at), deadline)
         if prologue is not None:
             at = jnp.where(prologue, -1, at)
@@ -283,6 +299,42 @@
         for action, at in timed:
             pl.when(at == now)(action)
 
+    def score(t, slot, first=0, count=None):
+        count = window_blocks if count is None else count
+        k = t // HALVES
+        half = t % HALVES
+        lanes = pl.ds(pl.multiple_of(half * half_width, half_width), half_width)
+        q = qbuf[k, :, lanes]
+        q = jnp.concatenate([q[:, h * HD:(h + 1) * HD] for h in range(PER_STEP)], axis=0)
+        scaled = q.astype(F32) * (LOG2E / math.sqrt(HD))
+        high = scaled.astype(BF16)
+        low = (scaled - high.astype(F32)).astype(BF16)
+        q = jnp.concatenate([high, low], axis=1)
+        k_rows = win[pl.ds(lane + off(k) + first, count), :, 0:HD].reshape(count * rows, HD)
+        k_rows = jnp.concatenate([k_rows, k_rows], axis=1)
+        part = lax.dot_general(q, k_rows, (((1,), (1,)), ((), ())), preferred_element_type=F32)
+        sbuf[slot, :, first * rows:(first + count) * rows] = part
+
+    def soft_part(slot, r, first, count):
+        scores = sbuf[slot, :, first * rows:(first + count) * rows].reshape(PER_STEP, rows, count * rows)
+        head, tail = rows if first == 0 else 0, rows if first + count == window_blocks else 0
+        parts = [scores[:, :, head:count * rows - tail]]
+        if head:
+            parts.insert(0, scores[:, :, :head] + bias[:, :rows][None])
+        if tail:
+            parts.append(scores[:, :, count * rows - tail:] + bias[:, rows:][None])
+        scores = jnp.concatenate(parts, axis=2)
+        top = jnp.max(scores, axis=-1, keepdims=True)
+        weights = jnp.exp2(scores - top).astype(BF16)
+        v_rows = win[pl.ds(r + first, count), :, HD:2 * HD].reshape(count * rows, HD)
+        v_rows = jnp.concatenate([v_rows, ones[pl.ds(r + first, count)].reshape(count * rows, HD)], axis=1)
+        weighted = jnp.dot(weights.reshape(PER_STEP * rows, count * rows), v_rows, preferred_element_type=F32)
+        return top.reshape(PER_STEP * rows, 1), weighted
+
+    def soften(t, slot):
+        _, weighted = soft_part(slot, lane + off(t // HALVES), 0, window_blocks)
+        wbuf[...] = weighted[:, :HD] / weighted[:, HD:]
+
     for k in (2, 3, 1):
         kv_quad(k).start()
     forward_kv(top_slot, 0, lambda copy: copy.start())
@@ -296,8 +348,6 @@
     for k in (1, 2, 3):
         q_quad(k).start()
 
-    window_blocks = reach + 1
-    keys = window_blocks * rows
     for edge, offset in ((0, reach * rows), (1, 0)):
         query = lax.broadcasted_iota(jnp.int32, (rows, rows), 0)
         key = lax.broadcasted_iota(jnp.int32, (rows, rows), 1) - offset
@@ -330,20 +380,14 @@
     take_z(top_slot - 2, 2)
     take_z(top_slot - 2, 3)
 
+    for slot in levels[1:]:
+        take_z(slot, 2)
+        take_z(slot, 3)
+
     @pl.when(has_up)
     def _():
         code_up(0).start()
-
-    @pl.when(y == 0)
-    def _():
-        send_y(z)
-    for slot in levels[1:]:
-        take_z(slot, 2)
-        take_z(slot, 3)
-
-    @pl.when(y == 1)
-    def _():
-        send_y(z)
+    send_y(z)
 
     run_events(-1)
     for slot in range(top_slot):
@@ -355,15 +399,30 @@
             for i in range(QUAD):
                 win[slot * QUAD + i] = fill
 
-    for slot in range(top_slot - 1, -1, -2):
+    late_blocks = 2 * QUAD
+
+    def take_y(slot):
         for k in range(QUAD):
             @pl.when(there(slot))
             def _():
                 level = (top_slot - 1 - slot) // 2
                 remote(block(slot, k), block(slot, k), ys.at[level, k], yr.at[level, k], me + dy).wait_recv()
+
+    for slot in range(top_slot - 1, 1, -2):
+        take_y(slot)
     own_q.wait()
     all_signs.wait()
     all_scales.wait()
+    score(0, 0, late_blocks, window_blocks - late_blocks)
+    near_top, near_sum = soft_part(0, lane, late_blocks, window_blocks - late_blocks)
+    tops[...] = jnp.broadcast_to(near_top, tops.shape)
+    sums[...] = near_sum
+    take_y(1)
+    score(0, 0, 0, late_blocks)
+    far_top, far_sum = soft_part(0, lane, 0, late_blocks)
+    both_top = jnp.maximum(tops[:, :1], far_top)
+    weighted = sums[...] * jnp.exp2(tops[:, :1] - both_top) + far_sum * jnp.exp2(far_top - both_top)
+    wbuf[...] = weighted[:, :HD] / weighted[:, HD:]
 
     def piece(r, source_lane, half):
         start = source_lane * width + half * half_width
@@ -396,38 +455,6 @@
         k = t // 2
         ref = piece(lane + dc + dx - (k % 2) * dc - (k // 2) * dx, lane + dc + dx, t % 2)
         return remote(ref, ref, rf_s.at[t], rf_r.at[t], me + dc)
-
-    first_edge, last_edge = rows, keys - rows
-
-    def score(t, slot):
-        k = t // HALVES
-        half = t % HALVES
-        lanes = pl.ds(pl.multiple_of(half * half_width, half_width), half_width)
-        q = qbuf[k, :, lanes]
-        q = jnp.concatenate([q[:, h * HD:(h + 1) * HD] for h in range(PER_STEP)], axis=0)
-        scaled = q.astype(F32) * (LOG2E / math.sqrt(HD))
-        high = scaled.astype(BF16)
-        low = (scaled - high.astype(F32)).astype(BF16)
-        q = jnp.concatenate([high, low], axis=1)
-        k_rows = win[pl.ds(lane + off(k), window_blocks), :, 0:HD].reshape(keys, HD)
-        k_rows = jnp.concatenate([k_rows, k_rows], axis=1)
-        sbuf[slot] = lax.dot_general(q, k_rows, (((1,), (1,)), ((), ())), preferred_element_type=F32)
-
-    def soften(t, slot):
-        r = lane + off(t // HALVES)
-        scores = sbuf[slot].reshape(PER_STEP, rows, keys)
-        scores = jnp.concatenate([
-            scores[:, :, :first_edge] + bias[:, :rows][None],
-            scores[:, :, first_edge:last_edge],
-            scores[:, :, last_edge:] + bias[:, rows:][None],
-        ], axis=2)
-        top = jnp.max(scores, axis=-1, keepdims=True)
-        weights = jnp.exp2(scores - top).astype(BF16)
-        v_rows = win[pl.ds(r, window_blocks), :, HD:2 * HD].reshape(keys, HD)
-        v_rows = jnp.concatenate([v_rows, ones[pl.ds(r, window_blocks)].reshape(keys, HD)], axis=1)
-        weighted = jnp.dot(weights.reshape(PER_STEP * rows, keys), v_rows, preferred_element_type=F32)
-        weighted = weighted[:, :HD] / weighted[:, HD:]
-        wbuf[...] = weighted
 
     def rotate(t):
         k = t // HALVES
@@ -444,34 +471,36 @@
         for h in range(PER_STEP):
             rot[lane + off(k), :, pl.ds(pl.multiple_of(start + h * HD, HD), HD)] = mixed[h * rows:(h + 1) * rows]
 
+    def publish(t):
+        @pl.when(me < n)
+        def _():
+            rotate(t)
+
+        @pl.when(t >= LAG)
+        def _():
+            rot_x_in(t - LAG).wait_recv()
+            rot_f(t - LAG).start()
+
+        run_events(t)
+        rot_x(t).start()
+        rot_c(t).start()
+
     def step(t, slot):
         score(jnp.minimum(t + 1, STEPS - 1), 1 - slot)
         soften(t, slot)
-
-        @pl.when(me < n)
-        def _():
-            rotate(t)
-
-        @pl.when(t >= LAG)
-        def _():
-            rot_x_in(t - LAG).wait_recv()
-            rot_f(t - LAG).start()
-
-        run_events(t)
-        rot_x(t).start()
-        rot_c(t).start()
-
-    def attend(k, carry):
-        step(k * HALVES, 0)
-
-        @pl.when(k < QUAD - 1)
-        def _():
-            remote(qbuf.at[k + 1], qbuf.at[k + 1], qs.at[k + 1], qr.at[k + 1], me + off(k + 1)).wait_recv()
-        step(k * HALVES + 1, 1)
+        publish(t)
+
+    def attend(j, carry):
+        k = j + 1
+        remote(qbuf.at[k], qbuf.at[k], qs.at[k], qr.at[k], me + off(k)).wait_recv()
+        step(2 * j + 1, 1)
+        step(2 * j + 2, 0)
         return carry
 
-    score(0, 0)
-    lax.fori_loop(0, QUAD, attend, 0)
+    publish(jnp.int32(0))
+    score(1, 1)
+    lax.fori_loop(0, QUAD - 1, attend, 0)
+    step(jnp.int32(STEPS - 1), 1)
     for t in range(STEPS - LAG, STEPS // 2):
         rot_x_in(t).wait_recv()
         rot_f(t).start()
@@ -616,11 +645,10 @@
     hbm = pl.BlockSpec(memory_space=pltpu.HBM)
     in_hbm = functools.partial(pltpu.with_memory_space_constraint, memory_space=pltpu.HBM)
     dma = pltpu.SemaphoreType.DMA
-    per_head = keys_values.reshape(rows, 2, KV, HD).transpose(2, 0, 1, 3).reshape(KV, rows, 2 * HD)
     return pl.pallas_call(
         functools.partial(kernel, n, reach, slots),
         out_shape=pltpu.VMEM((rows, n * cols), BF16),
-        in_specs=[hbm, vmem, hbm, vmem, hbm, hbm],
+        in_specs=[hbm, hbm, hbm, vmem, hbm, hbm],
         out_specs=pl.BlockSpec(memory_space=pl.ANY),
         scratch_shapes=[
             pltpu.VMEM((slots * QUAD, rows, 2 * HD), BF16),
@@ -631,11 +659,15 @@
             pltpu.VMEM((rows, 2 * rows), F32),
             pltpu.VMEM((2, PER_STEP * rows, (reach + 1) * rows), F32),
             pltpu.VMEM((PER_STEP * rows, HD), F32),
+            pltpu.VMEM((PER_STEP * rows, HD), F32),
+            pltpu.VMEM((PER_STEP * rows, 2 * HD), F32),
             pltpu.VMEM((2 * planes, QUAD, rows, cols), BF16),
             pltpu.VMEM((rows, HEADS * HD), BF16),
             pltpu.VMEM((STEPS, PER_STEP, HD), jnp.int32),
             pltpu.VMEM((HEADS, n * cols), BF16),
-            dma((6,)),
+            pltpu.VMEM((rows, 2, KV * HD), BF16),
+            pltpu.VMEM((KV, rows, 2 * HD), BF16),
+            dma((7,)),
             dma((QUAD,)), dma((QUAD,)),
             dma((QUAD,)), dma((QUAD,)),
             dma((slots // 2, QUAD)), dma((slots // 2, QUAD)),
@@ -655,7 +687,7 @@
         ),
     )(
         in_hbm(queries),
-        per_head,
+        in_hbm(keys_values),
         in_hbm(head_signs.reshape(STEPS, PER_STEP, HD)),
         reordered_hadamard(),
         in_hbm(out_codes),

time: 72.4 us -> 70.8 us (0.978)
  local copies, waits for them, and re-layouts: 2.52 us -> 1.32 us
    unnamed x3 -> x1, local copies, waits for them, and re-layouts: 2.17 us -> 1.32 us
where the time goes in v5:
time: 70.8 us; the launch traced here: 70.7 us
  Pallas kernels  69.2 us (98%)
  local copies, waits for them, and re-layouts  1.32 us (2%)
    pallas_call x1, Pallas kernels, on_device(): pl.pallas_call(functools.partial(kernel, n, reach, slots), out_shape=pltp...  69.2 us

profile of v5, /device:TPU:17, one launch (start us, length us, event | category | flops | bytes accessed | tf_op | source)
XLA Modules:
  0.0 70.7 jit_solution(6878198003471602338)
XLA Ops:
  0.0 0.1 select_convert_fusion.had_ref
  0.1 69.2 %shard_map.55 = bf16[128,8192]{1,0:T(8,128)(2,1)S(1)} custom-call(bf16[128,4096]{1,0:T(8,128)(2,1)} %q_ref.1, bf16[128,2,512]{2,1,0:T(2,128)(2,1)} %kv_ref.1, s32[8,4,128]{2,1,0:T(4,128)} %bitcast.1, bf16[128,128]{1,0:T(8,128)(2,1)S(1)} %select_convert_fusion.had_ref, s32[512,256]{1,0:T(8,128)} %codes_ref.1, bf16[32,8192]{1,0:T(8,128)(2,1)} %scales_ref.1), custom_call_target="tpu_custom_call" | custom-call | tf_op jit(solution)/shard_map/pallas_call | solution.py:648
  69.3 1.3 %copy.7 = bf16[128,8192]{1,0:T(8,128)(2,1)} copy(bf16[128,8192]{1,0:T(8,128)(2,1)S(1)} %shard_map.55) | data formatting | bytes 4194304
  (1 shorter events, 0.0 us)

commit v6 on v5

--- a/solution.py
+++ b/solution.py
@@ -111,18 +111,22 @@
     pl.semaphore_wait(barrier, QUAD + has_up.astype(jnp.int32) + has_down.astype(jnp.int32))
 
     own_kv.start()
+    def part_lanes(k):
+        return pl.ds((k % 2) * HD, HD)
+
     def block(slot, k):
-        return win.at[slot * QUAD + lane + off(k), :, pl.ds(0, 2 * HD)]
+        return win.at[slot * QUAD + lane + off(k // 2), :, part_lanes(k)]
 
     def kv_quad(k):
-        return remote(kv_heads.at[lane + off(k)], win.at[top_slot * QUAD + lane, :, pl.ds(0, 2 * HD)],
-                      kq_s.at[k], kq_r.at[k], me + off(k))
+        return remote(kv_heads.at[lane + off(k // 2), :, part_lanes(k)],
+                      win.at[top_slot * QUAD + lane, :, part_lanes(k)],
+                      kq_s.at[k], kq_r.at[k], me + off(k // 2))
 
     def kv_quad_in(k):
-        return remote(block(top_slot, k), block(top_slot, k), kq_s.at[k], kq_r.at[k], me + off(k))
+        return remote(block(top_slot, k), block(top_slot, k), kq_s.at[k], kq_r.at[k], me + off(k // 2))
 
     def source(slot, k):
-        return kv_heads.at[lane] if slot == top_slot and k == 0 else block(slot, k)
+        return kv_heads.at[lane, :, part_lanes(k)] if slot == top_slot and k < 2 else block(slot, k)
 
     def z_kv(slot, k):
         return remote(source(slot, k), block(slot - 2, k),
@@ -335,9 +339,10 @@
         _, weighted = soft_part(slot, lane + off(t // HALVES), 0, window_blocks)
         wbuf[...] = weighted[:, :HD] / weighted[:, HD:]
 
-    for k in (2, 3, 1):
+    for k in (4, 6, 2, 5, 7, 3):
         kv_quad(k).start()
-    forward_kv(top_slot, 0, lambda copy: copy.start())
+    for k in (0, 1):
+        forward_kv(top_slot, k, lambda copy: copy.start())
 
     own_codes.wait()
 
@@ -368,28 +373,32 @@
         forward_kv(slot, k, lambda copy: copy.start())
 
     levels = range(top_slot - 2, -1, -2)
-    take_quad(1)
+    for k in (2, 3):
+        take_quad(k)
     own_kv.wait()
-    take_z(top_slot - 2, 0)
-    take_z(top_slot - 2, 1)
-    take_quad(2)
-    take_quad(3)
+    for k in (0, 1, 2, 3):
+        take_z(top_slot - 2, k)
+    for k in (4, 6, 5, 7):
+        take_quad(k)
     for slot in levels[1:]:
-        take_z(slot, 0)
-        take_z(slot, 1)
-    take_z(top_slot - 2, 2)
-    take_z(top_slot - 2, 3)
+        for k in (0, 1, 2, 3):
+            take_z(slot, k)
+    for k in (4, 6, 5, 7):
+        take_z(top_slot - 2, k)
 
     for slot in levels[1:]:
-        take_z(slot, 2)
-        take_z(slot, 3)
+        for k in (4, 6, 5, 7):
+            take_z(slot, k)
 
     @pl.when(has_up)
     def _():
         code_up(0).start()
-    send_y(z)
-
-    run_events(-1)
+
+    def open_y():
+        send_y(z)
+        run_events(-1)
+
+    open_y()
     for slot in range(top_slot):
         @pl.when(jnp.logical_not(there(slot)))
         def _():
@@ -401,15 +410,15 @@
 
     late_blocks = 2 * QUAD
 
-    def take_y(slot):
-        for k in range(QUAD):
+    def take_y(slot, pieces):
+        for k in pieces:
             @pl.when(there(slot))
             def _():
                 level = (top_slot - 1 - slot) // 2
                 remote(block(slot, k), block(slot, k), ys.at[level, k], yr.at[level, k], me + dy).wait_recv()
 
     for slot in range(top_slot - 1, 1, -2):
-        take_y(slot)
+        take_y(slot, range(2 * QUAD))
     own_q.wait()
     all_signs.wait()
     all_scales.wait()
@@ -417,8 +426,9 @@
     near_top, near_sum = soft_part(0, lane, late_blocks, window_blocks - late_blocks)
     tops[...] = jnp.broadcast_to(near_top, tops.shape)
     sums[...] = near_sum
-    take_y(1)
+    take_y(1, range(0, 2 * QUAD, 2))
     score(0, 0, 0, late_blocks)
+    take_y(1, range(1, 2 * QUAD, 2))
     far_top, far_sum = soft_part(0, lane, 0, late_blocks)
     both_top = jnp.maximum(tops[:, :1], far_top)
     weighted = sums[...] * jnp.exp2(tops[:, :1] - both_top) + far_sum * jnp.exp2(far_top - both_top)
@@ -587,10 +597,11 @@
     lax.fori_loop(0, 4 * planes, sweep, 0)
 
     for k in (1, 2, 3):
+        q_quad(k).wait_send()
+    for k in range(2, 2 * QUAD):
         kv_quad(k).wait_send()
-        q_quad(k).wait_send()
     for slot in range(top_slot, -1, -2):
-        for k in range(QUAD):
+        for k in range(2 * QUAD):
             forward_kv(slot, k, lambda copy: copy.wait_send())
 
     def drain_codes(k, carry):
@@ -622,10 +633,17 @@
 
     lax.fori_loop(0, STEPS, drain_rot, 0)
 
-    def drain_out(unit, carry):
+    def drain_sent(unit, carry):
         out_own(unit).wait()
         for k in (1, 2, 3):
             out_send(unit, k).wait_send()
+        return carry
+
+    lax.fori_loop(0, 2 * planes, drain_sent, 0)
+
+    def drain_out(q, carry):
+        unit = plane_at(q // 2) * 2 + y + (q % 2) * (1 - 2 * y)
+        for k in (1, 2, 3):
             out_recv(unit, k).wait_recv()
         return carry
 
@@ -668,10 +686,10 @@
             pltpu.VMEM((rows, 2, KV * HD), BF16),
             pltpu.VMEM((KV, rows, 2 * HD), BF16),
             dma((7,)),
+            dma((2 * QUAD,)), dma((2 * QUAD,)),
             dma((QUAD,)), dma((QUAD,)),
-            dma((QUAD,)), dma((QUAD,)),
-            dma((slots // 2, QUAD)), dma((slots // 2, QUAD)),
-            dma((slots // 2, QUAD)), dma((slots // 2, QUAD)),
+            dma((slots // 2, 2 * QUAD)), dma((slots // 2, 2 * QUAD)),
+            dma((slots // 2, 2 * QUAD)), dma((slots // 2, 2 * QUAD)),
             dma((planes + 1,)), dma((planes + 1,)),
             dma((planes + 1,)), dma((planes + 1,)),
             dma((planes,)), dma((planes,)),

time: 70.8 us -> 69.8 us (0.986)
  Pallas kernels: 69.2 us -> 68.3 us
    pallas_call x1, Pallas kernels: 69.2 us -> 68.3 us  [on_device(): pl.pallas_call(functools.partial(kernel, n, reach, slots), out_shape=pltp...]
where the time goes in v6:
time: 69.8 us; the launch traced here: 69.7 us
  Pallas kernels  68.3 us (98%)
  local copies, waits for them, and re-layouts  1.32 us (2%)
    pallas_call x1, Pallas kernels, on_device(): pl.pallas_call(functools.partial(kernel, n, reach, slots), out_shape=pltp...  68.3 us

profile of v6, /device:TPU:17, one launch (start us, length us, event | category | flops | bytes accessed | tf_op | source)
XLA Modules:
  0.0 69.7 jit_solution(16562541098274236475)
XLA Ops:
  0.0 0.1 select_convert_fusion.had_ref
  0.1 68.3 %shard_map.55 = bf16[128,8192]{1,0:T(8,128)(2,1)S(1)} custom-call(bf16[128,4096]{1,0:T(8,128)(2,1)} %q_ref.1, bf16[128,2,512]{2,1,0:T(2,128)(2,1)} %kv_ref.1, s32[8,4,128]{2,1,0:T(4,128)} %bitcast.1, bf16[128,128]{1,0:T(8,128)(2,1)S(1)} %select_convert_fusion.had_ref, s32[512,256]{1,0:T(8,128)} %codes_ref.1, bf16[32,8192]{1,0:T(8,128)(2,1)} %scales_ref.1), custom_call_target="tpu_custom_call" | custom-call | tf_op jit(solution)/shard_map/pallas_call | solution.py:666
  68.4 1.3 %copy.7 = bf16[128,8192]{1,0:T(8,128)(2,1)} copy(bf16[128,8192]{1,0:T(8,128)(2,1)S(1)} %shard_map.55) | data formatting | bytes 4194304
  (1 shorter events, 0.0 us)

commit v7 on v6

--- a/solution.py
+++ b/solution.py
@@ -394,11 +394,12 @@
     def _():
         code_up(0).start()
 
-    def open_y():
-        send_y(z)
+    send_y(z)
+
+    @pl.when(z != 1)
+    def _():
         run_events(-1)
 
-    open_y()
     for slot in range(top_slot):
         @pl.when(jnp.logical_not(there(slot)))
         def _():
@@ -426,6 +427,10 @@
     near_top, near_sum = soft_part(0, lane, late_blocks, window_blocks - late_blocks)
     tops[...] = jnp.broadcast_to(near_top, tops.shape)
     sums[...] = near_sum
+
+    @pl.when(z == 1)
+    def _():
+        run_events(-1)
     take_y(1, range(0, 2 * QUAD, 2))
     score(0, 0, 0, late_blocks)
     take_y(1, range(1, 2 * QUAD, 2))

time: 69.8 us -> 69.9 us (level)
  no operation moved by 1% of the time
where the time goes in v7:
time: 69.9 us; the launch traced here: 69.7 us
  Pallas kernels  68.3 us (98%)
  local copies, waits for them, and re-layouts  1.32 us (2%)
    pallas_call x1, Pallas kernels, on_device(): pl.pallas_call(functools.partial(kernel, n, reach, slots), out_shape=pltp...  68.3 us

profile of v7, /device:TPU:17, one launch (start us, length us, event | category | flops | bytes accessed | tf_op | source)
XLA Modules:
  0.0 69.7 jit_solution(12477783526953428992)
XLA Ops:
  0.0 0.1 select_convert_fusion.had_ref
  0.1 68.3 %shard_map.55 = bf16[128,8192]{1,0:T(8,128)(2,1)S(1)} custom-call(bf16[128,4096]{1,0:T(8,128)(2,1)} %q_ref.1, bf16[128,2,512]{2,1,0:T(2,128)(2,1)} %kv_ref.1, s32[8,4,128]{2,1,0:T(4,128)} %bitcast.1, bf16[128,128]{1,0:T(8,128)(2,1)S(1)} %select_convert_fusion.had_ref, s32[512,256]{1,0:T(8,128)} %codes_ref.1, bf16[32,8192]{1,0:T(8,128)(2,1)} %scales_ref.1), custom_call_target="tpu_custom_call" | custom-call | tf_op jit(solution)/shard_map/pallas_call | solution.py:671
  68.4 1.3 %copy.7 = bf16[128,8192]{1,0:T(8,128)(2,1)} copy(bf16[128,8192]{1,0:T(8,128)(2,1)S(1)} %shard_map.55) | data formatting | bytes 4194304
  (1 shorter events, 0.0 us)
